TPU v7x, 256 devices: a whole 4x4x8 slice. The times are simulated.
256 devices in a mesh: bra: 16 (over z_lo, x), ket: 8 (over y, core), mpo: 2 (over z_hi).
Axes of the slice: x: 4, y: 4, z: 8 (z_hi: 2, z_lo: 4; z = z_hi * 4 + z_lo), core: 2. Of those that a mesh axis runs over, the one named last changes fastest.
Arguments:
- left_env: bfloat16 [4, 3072, 3072], P('mpo', 'bra', 'ket'), may hold values from -6 to 6
- site_tensor: bfloat16 [3072, 4, 3072], P('bra', None, 'ket'), may hold values from -0.0546875 to 0.0546875
- block_values: float32 [12, 4, 4], replicated, may hold values from -3 to 3
- pair_in: int32 [12], replicated, may hold values from 0 to 3
- pair_out: int32 [12], replicated, may hold values from 0 to 3, as said below
Outputs:
- new_env: bfloat16 [4, 3072, 3072], P('mpo', 'bra', 'ket')
Inputs may be any that keep to these rules, and one draw needn't show every extreme that they name: `pair_out`: every component number 0 to 3 appears at least once.
All inputs are finite; a program needn't handle non-finite values.
Results may differ from a plain program's by a relative error of at most 0.018.
Values may be sent and summed in bfloat16 or wider, within the bound.
No kernel may reach another device: no remote copies, remote signals or barrier semaphores. Data moves between devices by JAX's collectives and lax.ppermute only.
A program may use at most 64 MiB of HBM per device.

v0:
```python
import functools

import jax
import jax.numpy as jnp
from jax import lax
from jax.experimental import pallas as pl
from jax.experimental.pallas import tpu as pltpu
from jax.sharding import Mesh
from jax.sharding import PartitionSpec as P


AXES = ("zl", "x", "y", "core", "zh")
F32, BF16 = jnp.float32, jnp.bfloat16


def _zi(z):
    return (z % 4) * 2 + z // 4


def shift_z(v, k):
    return lax.ppermute(v, ("zl", "zh"), [(_zi(z), _zi((z + k) % 8)) for z in range(8)])


def shift_y(v, k):
    return lax.ppermute(v, "y", [(i, (i + k) % 4) for i in range(4)])


def flip_x(v, j):
    return lax.ppermute(v, "x", [(i, i ^ j) for i in range(4)])


def flip_z(v, j):
    return lax.ppermute(v, "zl", [(i, i ^ j) for i in range(4)])


def swap(v):
    return lax.ppermute(v, "core", [(0, 1), (1, 0)])


def call(body, outs, arrays, smem=(), scratch=(), mib=12, flops=0, nbytes=0):
    vm = pl.BlockSpec(memory_space=pltpu.VMEM)
    return pl.pallas_call(
        body,
        out_shape=outs,
        in_specs=[pl.BlockSpec(memory_space=pltpu.SMEM)] * len(smem) + [vm] * len(arrays),
        out_specs=jax.tree.map(lambda _: vm, outs),
        scratch_shapes=list(scratch),
        compiler_params=pltpu.CompilerParams(vmem_limit_bytes=mib * 1024 * 1024),
        cost_estimate=pl.CostEstimate(flops=flops, bytes_accessed=nbytes, transcendentals=0),
    )(*smem, *arrays)


def low_lanes(shape):
    return lax.broadcasted_iota(jnp.int32, shape, 1) < 64


def place():
    return [lax.axis_index(a) for a in AXES]


def prep_body(s_ref, _, *refs):
    outs, both = refs[:5], refs[5]
    zl, _, _, _, zh = place()

    def step(p, _):
        base = pl.multiple_of(p * 384, 384)

        def put(half, at, v):
            both[half, :, pl.ds(base + at, 128)] = v

        s0, s1 = s_ref.at[2 * p], s_ref.at[2 * p + 1]
        for half in range(2):
            main = slice(half * 256, half * 256 + 128)
            put(half, 0, s0[:, main])
            put(half, 128, s1[:, main])
        a, b = s0[:, 128:256].astype(F32), s1[:, 128:256].astype(F32)
        low = low_lanes(a.shape)
        put(0, 256, jnp.where(low, a, pltpu.roll(b, 64, 1)).astype(BF16))
        put(1, 256, jnp.where(low, pltpu.roll(a, 64, 1), b).astype(BF16))
        return 0

    lax.fori_loop(0, 2, step, 0)
    for i, out in enumerate(outs):
        lo, hi = ((0, 192), (0, 192), (0, 192), (0, 96), (96, 192))[i]
        dest = ((zh * 4 + zl + (0, 1, 7, 2, 6)[i]) % 8) // 4
        out[...] = both[dest, lo:hi]


def coef_body(bv, p_in, p_out, coef, mix):
    zh = place()[4]

    def zero(i, _):
        mix[i] = 0.0
        return 0

    lax.fori_loop(0, 256, zero, 0)

    def add(p, _):
        v = p_out[p]
        w = (p_in[p] + 2 * zh) % 4
        for s in range(4):
            for t in range(4):
                i = (v * 4 + s) * 16 + w * 4 + t
                mix[i] = mix[i] + bv[s, t, p]
        return 0

    lax.fori_loop(0, 12, add, 0)

    def main(i, _):
        rows = [jnp.full((1, 128), mix[i * 8 + k], F32) for k in range(8)]
        coef[pl.ds(pl.multiple_of(i * 8, 8), 8), :] = jnp.concatenate(rows, axis=0)
        return 0

    lax.fori_loop(0, 32, main, 0)
    low = low_lanes((1, 128))

    def half(i, _):
        rows = []
        for k in range(2):
            g = i * 2 + k
            vp, s, w = g // 16, (g // 4) % 4, g % 4
            for q in range(4):
                lo = mix[(2 * vp * 4 + s) * 16 + w * 4 + (0, 1, 2, 3)[q]]
                hi = mix[((2 * vp + 1) * 4 + s) * 16 + w * 4 + (1, 0, 3, 2)[q]]
                rows.append(jnp.where(low, jnp.full((1, 128), lo, F32), jnp.full((1, 128), hi, F32)))
        coef[pl.ds(pl.multiple_of(256 + i * 8, 8), 8), :] = jnp.concatenate(rows, axis=0)
        return 0

    lax.fori_loop(0, 16, half, 0)


def copy_body(*refs):
    out = refs[-1]
    for i, ref in enumerate(refs[:-1]):
        out[i] = ref[...]


def align_body(mine, other, out):
    zl, x, y, core, _ = place()
    parity, same = x % 2, (x // 2) == core

    def run(par, sm):
        def step(n, _):
            r = n // 4
            ry = (zl + r - y + 4) % 4
            part = pl.ds(pl.multiple_of((n % 4) * 96, 96), 96)
            for j in range(4):
                src = mine if ((j < 2) == sm) else other
                start = ((par + j) % 2) * 192
                out[j, r, part] = src[ry, part, start : start + 192]
            return 0

        lax.fori_loop(0, 16, step, 0)

    for par in range(2):
        for sm in range(2):
            pl.when((parity == par) & (same == (sm == 1)))(functools.partial(run, par, sm == 1))


def block(s, r, cols):
    own, near, far = s
    if r == 0:
        return own[:, cols]
    if r == 2:
        return far[:, cols]
    return near[r // 2, :, cols]


def products(e, s_of, js, cols):
    total = None
    for j in js:
        for r in range(4):
            d = jnp.dot(e[j, r], block(s_of[j], r, cols), preferred_element_type=F32)
            total = d if total is None else total + d
    return total


def inputs(refs):
    return {j: refs[3 * i : 3 * i + 3] for i, j in enumerate((0, 1, 3))}


def first_body(e, *refs):
    s_of, out = inputs(refs), refs[9]

    def n_step(n, _):
        cols = pl.ds(pl.multiple_of(n * 256, 256), 256)
        out[:, cols] = products(e, s_of, (0, 1, 3), cols)
        return 0

    lax.fori_loop(0, 3, n_step, 0)


def half_body(coef, part, e0, e1, *refs):
    s_of = inputs(refs)
    s_of[2] = (refs[9].at[0], refs[10], refs[9].at[1])
    out, acc = refs[11], refs[12]

    def n_step(n, _):
        cols = pl.ds(pl.multiple_of(n * 256, 256), 256)
        acc[1, :, cols] = products(e1, s_of, (0, 1, 3, 2), cols)
        acc[0, :, cols] = part[:, cols] + products(e0, s_of, (2,), cols)
        return 0

    lax.fori_loop(0, 3, n_step, 0)

    tile_of = (0, 1, 3, 4)
    rows = 16

    def a_step(i, _):
        a0 = pl.multiple_of(i * rows, rows)

        def tile(w, k):
            return acc[w // 2, pl.ds((w % 2) * 192 + a0, rows), k * 128 : (k + 1) * 128]

        for v in range(4):
            lane = (v // 2) * 384 + (v % 2) * 128
            totals = [None] * 4
            for w in range(4):
                for t in range(4):
                    x = tile(w, tile_of[t])
                    for s in range(4):
                        idx = (v * 4 + s) * 16 + w * 4 + t
                        d = coef[idx : idx + 1, :] * x
                        totals[s] = d if totals[s] is None else totals[s] + d
            for s in range(4):
                out[pl.ds(s * 192 + a0, rows), lane : lane + 128] = totals[s].astype(BF16)
        totals = [None] * 8
        for w in range(4):
            for q in range(4):
                x = tile(w, 2 if q < 2 else 5)
                if q % 2:
                    x = pltpu.roll(x, 64, 1)
                for vs in range(8):
                    idx = 256 + vs * 16 + w * 4 + q
                    d = coef[idx : idx + 1, :] * x
                    totals[vs] = d if totals[vs] is None else totals[vs] + d
        for vs in range(8):
            lane = (vs // 4) * 384 + 256
            out[pl.ds((vs % 4) * 192 + a0, rows), lane : lane + 128] = totals[vs].astype(BF16)
        return 0

    lax.fori_loop(0, 192 // rows, a_step, 0)


def terms_of(js, rows, m_ref, mine, other, write):
    _, x, y, core, _ = place()
    same = (x // 2) == core

    def run(sm):
        def step(zl, _):
            ry = (zl - y + 4) % 4
            for j in js:
                src = mine if ((j < 2) == sm) else other
                lo, hi = rows(j)
                row0 = pl.multiple_of(((x + j) % 2) * 192 + lo, 96)
                d = jnp.dot(
                    src[ry, pl.ds(row0, hi - lo), :], m_ref[...], preferred_element_type=F32
                ).astype(BF16)
                write(j, zl, d)
            return 0

        lax.fori_loop(0, 4, step, 0)

    for sm in range(2):
        pl.when(same == (sm == 1))(functools.partial(run, sm == 1))


def term2_body(m_ref, mine, other, ra, rb):
    def write(j, zl, d):
        ra[zl], rb[zl] = d[:48], d[48:]

    terms_of((2,), lambda j: (0, 96), m_ref, mine, other, write)


def term_body(m_ref, mine, other, m1, m3, s1b, s3b, t1, t3):
    def write(j, zl, d):
        if j == 2:
            m1[1, zl], m3[1, zl] = d[:48], d[48:]
        elif j == 1:
            m1[0, zl], s1b[zl] = d[0:48], d[96:144]
            t1[0, zl], t1[1, zl] = d[48:96], d[144:192]
        else:
            m3[0, zl], s3b[zl] = d[48:96], d[144:192]
            t3[0, zl], t3[1, zl] = d[0:48], d[96:144]

    def rows(j):
        return (96, 192) if j == 2 else (0, 192)

    terms_of((2, 1, 3), rows, m_ref, mine, other, write)


def term0_body(m_ref, mine, other, o0):
    def write(j, zl, d):
        o0[zl] = d

    terms_of((0,), lambda j: (0, 192), m_ref, mine, other, write)


def add_body(a, ra, b, rb, oa, ob):
    oa[...] = (a[0].astype(F32) + ra[...].astype(F32)).astype(BF16)
    ob[...] = (b[0].astype(F32) + rb[...].astype(F32)).astype(BF16)


def add2_body(a, ra, b, rb, oa, ob):
    oa[...] = (a[1].astype(F32) + ra[1].astype(F32)).astype(BF16)
    ob[...] = (b[1].astype(F32) + rb[1].astype(F32)).astype(BF16)


def se_body(s0, s1, c, d, s3, out):
    out[0], out[1], out[3] = s0[...], s1[...], s3[...]
    out[2, :192], out[2, 192:] = c[...], d[...]


def split_body(a, b, oa, ob):
    oa[...], ob[...] = a[:192], b[192:]


def join_body(a, b, out):
    out[:96], out[96:] = a[...], b[...]


def zprep0_body(o0, m1, t3, m3, t1, *outs):
    zl0 = place()[0]
    for k in range(4):
        zl = zl0 ^ k
        for q, (u, v) in enumerate(((m1.at[0], t3), (m3.at[0], t1))):
            own = o0[zl, q * 48 : (q + 1) * 48]
            outs[k][48 * q : 48 * (q + 1)] = (
                own.astype(F32) + u[zl].astype(F32) + v[zl].astype(F32)
            ).astype(BF16)


def zsum_body(a, b, c, d, keep, give):
    zh = place()[4]

    def run(half):
        for h in range(2):
            cols = slice(h * 384, (h + 1) * 384)
            total = a[:, cols].astype(F32)
            for r in (b, c, d):
                total = total + r[:, cols].astype(F32)
            if h == half:
                keep[...] = total
            else:
                give[...] = total.astype(BF16)

    for half in range(2):
        pl.when(zh == half)(functools.partial(run, half))


def zlast_body(o0, s1, t3, s3, t1, *outs):
    zl0, _, _, _, zh = place()
    for k in range(8):
        z = (zh * 4 + zl0 + k) % 8
        zl = z % 4
        lane = pl.ds(pl.multiple_of((z // 4) * 384, 128), 384)
        for q, (u, v) in enumerate(((s1, t3), (s3, t1))):
            own = o0[zl, (2 + q) * 48 : (3 + q) * 48, lane]
            outs[k][48 * q : 48 * (q + 1)] = (
                own.astype(F32) + u[zl, :, lane].astype(F32) + v[zl, :, lane].astype(F32)
            ).astype(BF16)


def final_body(keep, give, *refs):
    ins, out = refs[:8], refs[8]
    zl0, _, _, _, zh = place()
    z0 = zh * 4 + zl0

    def write(row0, i, a0, a1):
        rows = pl.ds(pl.multiple_of(row0 + i * 32, 32), 32)
        h0, h1 = a0[:, 256:], a1[:, 256:]
        low = low_lanes(h0.shape)
        out[0, rows, 0:128] = a0[:, 0:128].astype(BF16)
        out[1, rows, 0:128] = a0[:, 128:256].astype(BF16)
        out[0, rows, 128:256] = jnp.where(low, h0, pltpu.roll(h1, 64, 1)).astype(BF16)
        out[1, rows, 128:256] = jnp.where(low, pltpu.roll(h0, 64, 1), h1).astype(BF16)
        out[0, rows, 256:384] = a1[:, 0:128].astype(BF16)
        out[1, rows, 256:384] = a1[:, 128:256].astype(BF16)

    def step(i, _):
        part = pl.ds(pl.multiple_of(i * 32, 32), 32)
        kept, got = keep[part], give[part].astype(F32)
        first = zh == 0
        write(0, i, jnp.where(first, kept, got), jnp.where(first, got, kept))
        a0 = jnp.zeros((32, 384), F32)
        a1 = jnp.zeros((32, 384), F32)
        for k in range(8):
            v = ins[k][part].astype(F32)
            low_z = ((z0 + 8 - k) % 8) < 4
            a0 = a0 + jnp.where(low_z, v, 0.0)
            a1 = a1 + jnp.where(low_z, 0.0, v)
        write(96, i, a0, a1)
        return 0

    lax.fori_loop(0, 3, step, 0)


def sds(*shape, dtype=BF16):
    return jax.ShapeDtypeStruct(shape, dtype)


def program(left_env, site_tensor, block_values, pair_in, pair_out):
    env = left_env.reshape(384, 384)
    st = jnp.transpose(site_tensor, (1, 0, 2))
    set_ = jnp.transpose(st.reshape(768, 384))
    ea = shift_y(env, -1)
    eb = shift_y(env, 1)
    a_own, a_p, a_m, a_p2, a_m2 = call(
        prep_body,
        [sds(192, 768), sds(192, 768), sds(192, 768), sds(96, 768), sds(96, 768)],
        [st, set_],
        scratch=[pltpu.VMEM((2, 192, 768), BF16)],
        nbytes=4 << 20,
    )
    za = shift_z(a_m, -1)
    zb = shift_z(a_p, 1)
    zc = shift_z(a_p2, 2)
    zd = shift_z(a_m2, -2)
    xa1 = flip_x(a_own, 1)
    xa3 = flip_x(a_own, 3)
    ec = shift_y(env, 2)
    ez = shift_z(env, 4)
    sa = shift_y(set_, -1)
    sb = shift_y(set_, 1)
    near = call(copy_body, sds(2, 192, 768), [za, zb], nbytes=1 << 20)
    xb1 = flip_x(near, 1)
    xb3 = flip_x(near, 3)
    far = call(join_body, sds(192, 768), [zc, zd], nbytes=1 << 20)
    xc1 = flip_x(far, 1)
    xc3 = flip_x(far, 3)
    e_own = call(copy_body, sds(4, 384, 384), [env, ea, ec, eb], nbytes=2 << 20)
    e_own_s = swap(e_own)
    coef = call(
        coef_body,
        sds(384, 128, dtype=F32),
        [],
        smem=[jnp.transpose(block_values, (1, 2, 0)), pair_in, pair_out],
        scratch=[pltpu.SMEM((256,), F32)],
        nbytes=1 << 20,
    )
    fa = shift_y(ez, -1)
    fb = shift_y(ez, 1)
    fc = shift_y(ez, 2)
    e0 = call(align_body, sds(4, 4, 384, 192), [e_own, e_own_s], nbytes=8 << 20)
    sa2, sb2 = call(split_body, [sds(192, 768)] * 2, [sa, sb], nbytes=1 << 20)
    sc = shift_y(sa2, -1)
    sd = shift_y(sb2, 1)
    xf13 = flip_x(xb3, 1)
    pair = call(copy_body, sds(2, 192, 768), [xa1, xc1], nbytes=1 << 20)
    xf02 = flip_x(pair, 3)
    s_in = [a_own, near, far, xa1, xb1, xc1, xa3, xb3, xc3]
    part = call(
        first_body,
        sds(384, 768, dtype=F32),
        [e0, *s_in],
        flops=2 * 384 * 768 * 2304,
        nbytes=8 << 20,
    )
    e_oth = call(copy_body, sds(4, 384, 384), [ez, fa, fc, fb], nbytes=2 << 20)
    e_oth_s = swap(e_oth)
    e1 = call(align_body, sds(4, 4, 384, 192), [e_oth, e_oth_s], nbytes=8 << 20)
    se = call(se_body, sds(4, 384, 768), [set_, sa, sc, sd, sb], nbytes=6 << 20)
    se_s = swap(se)
    mixed = call(
        half_body,
        sds(768, 768),
        [coef, part, e0, e1, *s_in, xf02, xf13],
        scratch=[pltpu.VMEM((2, 384, 768), F32)],
        mib=20,
        flops=2 * 384 * 768 * 3840,
        nbytes=12 << 20,
    )
    qt, q2 = sds(4, 48, 768), sds(2, 4, 48, 768)
    args = [mixed, se, se_s]
    ra, rb = call(term2_body, [qt, qt], args, mib=16, flops=1 << 30, nbytes=4 << 20)
    r1 = flip_x(ra, 1)
    r3 = flip_x(rb, 3)
    m1, m3, s1b, s3b, t1q, t3q = call(
        term_body, [q2, q2, qt, qt, q2, q2], args, mib=16, flops=1 << 31, nbytes=8 << 20
    )
    m1 = flip_x(m1, 1)
    m3 = flip_x(m3, 3)
    ta, tb = call(add_body, [qt, qt], [t3q, r1, t1q, r3], nbytes=2 << 20)
    t3, t1 = [None] * 2, [None] * 2
    t3[0] = flip_x(ta, 3)
    t1[0] = flip_x(tb, 1)
    s1b = flip_x(s1b, 1)
    s3b = flip_x(s3b, 3)
    ta, tb = call(add2_body, [qt, qt], [t3q, m1, t1q, m3], nbytes=2 << 20)
    t3[1] = flip_x(ta, 3)
    t1[1] = flip_x(tb, 1)
    (o0,) = call(term0_body, [sds(4, 192, 768)], args, mib=16, flops=1 << 30, nbytes=6 << 20)
    got = call(zprep0_body, [sds(96, 768)] * 4, [o0, m1, t3[0], m3, t1[0]], nbytes=4 << 20)
    got = [got[0]] + [flip_z(got[k], k) for k in (1, 2, 3)]
    last = call(zlast_body, [sds(96, 384)] * 8, [o0, s1b, t3[1], s3b, t1[1]], nbytes=4 << 20)
    last = [last[0]] + [shift_z(last[k], k) for k in range(1, 8)]
    keep, give = call(zsum_body, [sds(96, 384, dtype=F32), sds(96, 384)], got, nbytes=1 << 20)
    give = shift_z(give, 4)
    return call(final_body, sds(2, 192, 384), [keep, give, *last], nbytes=2 << 20)


def solution(mesh):
    finer = Mesh(mesh.devices.reshape(4, 4, 4, 2, 2), AXES)
    return jax.shard_map(
        program,
        mesh=finer,
        in_specs=(P("zh", ("zl", "x"), ("y", "core")), P(("zl", "x"), None, ("y", "core")), P(), P(), P()),
        out_specs=P("zh", ("zl", "x"), ("y", "core")),
        check_vma=False,
    )
```

profile of v0, /device:TPU:4, one launch (start us, length us, event | category | flops | bytes accessed | tf_op | source)
XLA Modules:
  0.0 200.0 jit_solution(4894587357497831928)
XLA Ops:
  4.5 12.6 %collective-permute-done.21.a.s1 = bf16[384,768]{1,0:T(8,128)(2,1)S(1)} collective-permute-done((bf16[384,768]{1,0:T(8,128)(2,1)S(1)}, bf16[384,768]{1,0:T(8,128)(2,1)S(1)}, u32[]{:S(2)}, u32[]{:S(2)}) %collective-permute-start.21) | collective-permute-done | bytes 589856 | tf_op jit(solution)/shard_map/ppermute | solution.py:25
  17.1 3.4 %collective-permute-done.22.b.s3 = bf16[384,768]{1,0:T(8,128)(2,1)S(1)} collective-permute-done((bf16[384,768]{1,0:T(8,128)(2,1)S(1)}, bf16[384,768]{1,0:T(8,128)(2,1)S(1)}, u32[]{:S(2)}, u32[]{:S(2)}) %collective-permute-start.22) | collective-permute-done | bytes 589856 | tf_op jit(solution)/shard_map/ppermute | solution.py:25
  24.5 3.3 %collective-permute-start.6 = (bf16[96,768]{1,0:T(8,128)(2,1)S(1)}, bf16[96,768]{1,0:T(8,128)(2,1)S(1)}, u32[]{:S(2)}, u32[]{:S(2)}) collective-permute-start(bf16[96,768]{1,0:T(8,128)(2,1)S(1)} %get-tuple-element.41), channel_id=1, source_target_pairs={{0,128},{64,192},{128,1},{192,65},{1,129},{65,193},{129,0},{193,64... | collective-permute-start | bytes 442376 | tf_op jit(solution)/shard_map/ppermute | solution.py:21
  27.8 3.1 %collective-permute-start.7 = (bf16[96,768]{1,0:T(8,128)(2,1)S(1)}, bf16[96,768]{1,0:T(8,128)(2,1)S(1)}, u32[]{:S(2)}, u32[]{:S(2)}) collective-permute-start(bf16[96,768]{1,0:T(8,128)(2,1)S(1)} %get-tuple-element.42), channel_id=1, source_target_pairs={{0,129},{64,193},{128,0},{192,64},{1,128},{65,192},{129,1},{193,65... | collective-permute-start | bytes 442376 | tf_op jit(solution)/shard_map/ppermute | solution.py:21
  31.8 3.7 %collective-permute-done.6.a = bf16[96,768]{1,0:T(8,128)(2,1)S(1)} collective-permute-done((bf16[96,768]{1,0:T(8,128)(2,1)S(1)}, bf16[96,768]{1,0:T(8,128)(2,1)S(1)}, u32[]{:S(2)}, u32[]{:S(2)}) %collective-permute-start.6) | collective-permute-done | bytes 147488 | tf_op jit(solution)/shard_map/ppermute | solution.py:21
  35.4 4.9 %collective-permute-start.14 = (bf16[384,384]{1,0:T(8,128)(2,1)S(1)}, bf16[384,384]{1,0:T(8,128)(2,1)S(1)}, u32[]{:S(2)}, u32[]{:S(2)}) collective-permute-start(bf16[384,384]{1,0:T(8,128)(2,1)S(1)} %bitcast.15), channel_id=1, source_target_pairs={{0,1},{64,65},{128,129},{192,193},{1,0},{65,64},{129,128},{193,192... | collective-permute-start | bytes 884744 | tf_op jit(solution)/shard_map/ppermute | solution.py:21
  42.7 10.7 %collective-permute-done.14.refs_0_ = bf16[384,384]{1,0:T(8,128)(2,1)S(1)} collective-permute-done((bf16[384,384]{1,0:T(8,128)(2,1)S(1)}, bf16[384,384]{1,0:T(8,128)(2,1)S(1)}, u32[]{:S(2)}, u32[]{:S(2)}) %collective-permute-start.14) | collective-permute-done | bytes 294944 | tf_op jit(solution)/shard_map/ppermute | solution.py:21
  55.7 3.4 %collective-permute-done.4.refs_0_ = bf16[192,768]{1,0:T(8,128)(2,1)S(1)} collective-permute-done((bf16[192,768]{1,0:T(8,128)(2,1)S(1)}, bf16[192,768]{1,0:T(8,128)(2,1)S(1)}, u32[]{:S(2)}, u32[]{:S(2)}) %collective-permute-start.4) | collective-permute-done | bytes 294944 | tf_op jit(solution)/shard_map/ppermute | solution.py:21
  62.6 7.0 %collective-permute-done.17.refs_3_ = bf16[384,384]{1,0:T(8,128)(2,1)S(1)} collective-permute-done((bf16[384,384]{1,0:T(8,128)(2,1)S(1)}, bf16[384,384]{1,0:T(8,128)(2,1)S(1)}, u32[]{:S(2)}, u32[]{:S(2)}) %collective-permute-start.17) | collective-permute-done | bytes 294944 | tf_op jit(solution)/shard_map/ppermute | solution.py:25
  71.5 6.8 %collective-permute-done.10.refs_5_.refs_1_ = bf16[192,768]{1,0:T(8,128)(2,1)S(1)} collective-permute-done((bf16[192,768]{1,0:T(8,128)(2,1)S(1)}, bf16[192,768]{1,0:T(8,128)(2,1)S(1)}, u32[]{:S(2)}, u32[]{:S(2)}) %collective-permute-start.10) | collective-permute-done | bytes 294944 | tf_op jit(solution)/shard_map/ppermute | solution.py:29
  78.8 13.3 %collective-permute-done.13.refs_8_ = bf16[192,768]{1,0:T(8,128)(2,1)S(1)} collective-permute-done((bf16[192,768]{1,0:T(8,128)(2,1)S(1)}, bf16[192,768]{1,0:T(8,128)(2,1)S(1)}, u32[]{:S(2)}, u32[]{:S(2)}) %collective-permute-start.13) | collective-permute-done | bytes 294944 | tf_op jit(solution)/shard_map/ppermute | solution.py:29
  95.4 4.3 %shard_map.55.coef = f32[384,128]{1,0:T(8,128)S(1)} custom-call(f32[4,4,12]{2,1,0:T(4,128)S(1)} %bitcast.18, s32[12]{0:T(128)S(1)} %copy-done.2, s32[12]{0:T(128)S(1)} %copy-done.3), custom_call_target="tpu_custom_call" | custom-call | bytes 1048576 | tf_op jit(solution)/shard_map/pallas_call | solution.py:42
  101.5 6.8 %collective-permute-done.9.refs_4_ = bf16[2,192,768]{2,1,0:T(8,128)(2,1)S(1)} collective-permute-done((bf16[2,192,768]{2,1,0:T(8,128)(2,1)S(1)}, bf16[2,192,768]{2,1,0:T(8,128)(2,1)S(1)}, u32[]{:S(2)}, u32[]{:S(2)}) %collective-permute-start.9) | collective-permute-done | bytes 589856 | tf_op jit(solution)/shard_map/ppermute | solution.py:29
  112.4 6.4 %collective-permute-done.20.refs_10_ = bf16[2,192,768]{2,1,0:T(8,128)(2,1)S(1)} collective-permute-done((bf16[2,192,768]{2,1,0:T(8,128)(2,1)S(1)}, bf16[2,192,768]{2,1,0:T(8,128)(2,1)S(1)}, u32[]{:S(2)}, u32[]{:S(2)}) %collective-permute-start.20) | collective-permute-done | bytes 589856 | tf_op jit(solution)/shard_map/ppermute | solution.py:29
  118.8 6.1 %shard_map.65.m_ref = bf16[768,768]{1,0:T(8,128)(2,1)S(1)} custom-call(f32[384,128]{1,0:T(8,128)S(1)} %shard_map.55.coef, f32[384,768]{1,0:T(8,128)S(1)} %shard_map.61.part, bf16[4,4,384,192]{3,2,1,0:T(8,128)(2,1)S(1)} %shard_map.57.e.e0, bf16[4,4,384,192]{3,2,1,0:T(8,128)(2,1)S(1)} %shard_map.63.e1, bf16[192,768]{1,0:T(8,128)(2,1)S(1)} %get-tuple-element.38.refs_0_, ...), custom_call_target="tpu_custom_call" | custom-call | flops 2264924160 | bytes 12582912 | tf_op jit(solution)/shard_map/pallas_call | solution.py:42
  128.6 3.2 %shard_map.69 = (bf16[2,4,48,768]{3,2,1,0:T(8,128)(2,1)S(1)}, bf16[2,4,48,768]{3,2,1,0:T(8,128)(2,1)S(1)}, bf16[4,48,768]{2,1,0:T(8,128)(2,1)S(1)}, bf16[4,48,76...) custom-call(bf16[768,768]{1,0:T(8,128)(2,1)S(1)} %shard_map.65.m_ref, ...), custom_call_target="tpu_custom_call" | custom-call | flops 2147483648 | bytes 8388608 | tf_op jit(solution)/shard_map/pallas_call | solution.py:42
  140.2 7.8 %collective-permute-done.26.m1.ra = bf16[2,4,48,768]{3,2,1,0:T(8,128)(2,1)S(1)} collective-permute-done((bf16[2,4,48,768]{3,2,1,0:T(8,128)(2,1)S(1)}, bf16[2,4,48,768]{3,2,1,0:T(8,128)(2,1)S(1)}, u32[]{:S(2)}, u32[]{:S(2)}) %collective-permute-start.26) | collective-permute-done | bytes 589856 | tf_op jit(solution)/shard_map/ppermute | solution.py:29
  149.7 4.0 %collective-permute-done.29.t3 = bf16[4,48,768]{2,1,0:T(8,128)(2,1)S(1)} collective-permute-done((bf16[4,48,768]{2,1,0:T(8,128)(2,1)S(1)}, bf16[4,48,768]{2,1,0:T(8,128)(2,1)S(1)}, u32[]{:S(2)}, u32[]{:S(2)}) %collective-permute-start.29) | collective-permute-done | bytes 294944 | tf_op jit(solution)/shard_map/ppermute | solution.py:29
  162.4 3.1 %collective-permute-done.33.c = bf16[96,768]{1,0:T(8,128)(2,1)S(1)} collective-permute-done((bf16[96,768]{1,0:T(8,128)(2,1)S(1)}, bf16[96,768]{1,0:T(8,128)(2,1)S(1)}, u32[]{:S(2)}, u32[]{:S(2)}) %collective-permute-start.33) | collective-permute-done | bytes 147488 | tf_op jit(solution)/shard_map/ppermute | solution.py:33
  166.0 6.4 %collective-permute-done.34.d = bf16[96,768]{1,0:T(8,128)(2,1)S(1)} collective-permute-done((bf16[96,768]{1,0:T(8,128)(2,1)S(1)}, bf16[96,768]{1,0:T(8,128)(2,1)S(1)}, u32[]{:S(2)}, u32[]{:S(2)}) %collective-permute-start.34) | collective-permute-done | bytes 147488 | tf_op jit(solution)/shard_map/ppermute | solution.py:33
  172.5 6.1 %collective-permute-start.35 = (bf16[96,384]{1,0:T(8,128)(2,1)S(1)}, bf16[96,384]{1,0:T(8,128)(2,1)S(1)}, u32[]{:S(2)}, u32[]{:S(2)}) collective-permute-start(bf16[96,384]{1,0:T(8,128)(2,1)S(1)} %get-tuple-element.58), channel_id=1, source_target_pairs={{0,1},{64,65},{128,129},{192,193},{1,0},{65,64},{129,128},{193,192... | collective-permute-start | bytes 221192 | tf_op jit(solution)/shard_map/ppermute | solution.py:21
  179.0 5.9 %collective-permute-start.41 = (bf16[96,384]{1,0:T(8,128)(2,1)S(1)}, bf16[96,384]{1,0:T(8,128)(2,1)S(1)}, u32[]{:S(2)}, u32[]{:S(2)}) collective-permute-start(bf16[96,384]{1,0:T(8,128)(2,1)S(1)} %get-tuple-element.65), channel_id=1, source_target_pairs={{0,128},{64,192},{128,1},{192,65},{1,129},{65,193},{129,0},{193,64... | collective-permute-start | bytes 221192 | tf_op jit(solution)/shard_map/ppermute | solution.py:21
  185.5 4.4 %collective-permute-start.44 = (bf16[96,384]{1,0:T(8,128)(2,1)S(1)}, bf16[96,384]{1,0:T(8,128)(2,1)S(1)}, u32[]{:S(2)}, u32[]{:S(2)}) collective-permute-start(bf16[96,384]{1,0:T(8,128)(2,1)S(1)} %get-tuple-element.68), channel_id=1, source_target_pairs={{0,65},{64,129},{128,193},{192,0},{1,64},{65,128},{129,192},{193,1... | collective-permute-start | bytes 221192 | tf_op jit(solution)/shard_map/ppermute | solution.py:21
  189.9 3.5 %collective-permute-start.45 = (bf16[96,384]{1,0:T(8,128)(2,1)S(1)}, bf16[96,384]{1,0:T(8,128)(2,1)S(1)}, u32[]{:S(2)}, u32[]{:S(2)}) collective-permute-start(bf16[96,384]{1,0:T(8,128)(2,1)S(1)} %get-tuple-element.69), channel_id=1, source_target_pairs={{0,129},{64,193},{128,0},{192,64},{1,128},{65,192},{129,1},{193,65... | collective-permute-start | bytes 221192 | tf_op jit(solution)/shard_map/ppermute | solution.py:21
  (102 shorter events, 59.4 us)
Async XLA Ops:
  1.4 15.7 %collective-permute-start.21 = (bf16[384,768]{1,0:T(8,128)(2,1)S(1)}, bf16[384,768]{1,0:T(8,128)(2,1)S(1)}, u32[]{:S(2)}, u32[]{:S(2)}) collective-permute-start(bf16[384,768]{1,0:T(8,128)(2,1)S(1)} %bitcast.7), channel_id=1, source_target_pairs={{0,12},{4,0},{8,4},{12,8},{1,13},{5,1},{9,5},{13,9},{2,14},{6,2},{... | collective-permute-start | bytes 1769480 | tf_op jit(solution)/shard_map/ppermute | solution.py:25
  4.5 16.0 %collective-permute-start.22 = (bf16[384,768]{1,0:T(8,128)(2,1)S(1)}, bf16[384,768]{1,0:T(8,128)(2,1)S(1)}, u32[]{:S(2)}, u32[]{:S(2)}) collective-permute-start(bf16[384,768]{1,0:T(8,128)(2,1)S(1)} %bitcast.8), channel_id=1, source_target_pairs={{0,4},{4,8},{8,12},{12,0},{1,5},{5,9},{9,13},{13,1},{2,6},{6,10},{... | collective-permute-start | bytes 1769480 | tf_op jit(solution)/shard_map/ppermute | solution.py:25
  22.7 17.9 %collective-permute-start = (bf16[384,384]{1,0:T(8,128)(2,1)S(1)}, bf16[384,384]{1,0:T(8,128)(2,1)S(1)}, u32[]{:S(2)}, u32[]{:S(2)}) collective-permute-start(bf16[384,384]{1,0:T(8,128)(2,1)S(1)} %bitcast.13), channel_id=1, source_target_pairs={{0,12},{4,0},{8,4},{12,8},{1,13},{5,1},{9,5},{13,9},{2,14},{6,2},{... | collective-permute-start | bytes 884744 | tf_op jit(solution)/shard_map/ppermute | solution.py:25
  31.7 93.2 %collective-permute-start.25 = (bf16[4,384,768]{2,1,0:T(8,128)(2,1)S(1)}, bf16[4,384,768]{2,1,0:T(8,128)(2,1)S(1)}, u32[]{:S(2)}, u32[]{:S(2)}) collective-permute-start(bf16[4,384,768]{2,1,0:T(8,128)(2,1)S(1)} %shard_map.67.mine), channel_id=1, source_target_pairs={{0,2},{2,0},{1,3},{3,1},{4,6},{6,4},{5,7},{7,5},{8,10},{10,8},{9,1... | collective-permute-start | bytes 7077896 | tf_op jit(solution)/shard_map/ppermute | solution.py:37
  35.4 17.9 %collective-permute-start.14 = (bf16[384,384]{1,0:T(8,128)(2,1)S(1)}, bf16[384,384]{1,0:T(8,128)(2,1)S(1)}, u32[]{:S(2)}, u32[]{:S(2)}) collective-permute-start(bf16[384,384]{1,0:T(8,128)(2,1)S(1)} %bitcast.15), channel_id=1, source_target_pairs={{0,1},{64,65},{128,129},{192,193},{1,0},{65,64},{129,128},{193,192... | collective-permute-start | bytes 884744 | tf_op jit(solution)/shard_map/ppermute | solution.py:21
  40.4 13.3 %collective-permute-start.2 = (bf16[384,384]{1,0:T(8,128)(2,1)S(1)}, bf16[384,384]{1,0:T(8,128)(2,1)S(1)}, u32[]{:S(2)}, u32[]{:S(2)}) collective-permute-start(bf16[384,384]{1,0:T(8,128)(2,1)S(1)} %bitcast.16), channel_id=1, source_target_pairs={{0,4},{4,8},{8,12},{12,0},{1,5},{5,9},{9,13},{13,1},{2,6},{6,10},{... | collective-permute-start | bytes 884744 | tf_op jit(solution)/shard_map/ppermute | solution.py:25
  40.6 18.4 %collective-permute-start.4 = (bf16[192,768]{1,0:T(8,128)(2,1)S(1)}, bf16[192,768]{1,0:T(8,128)(2,1)S(1)}, u32[]{:S(2)}, u32[]{:S(2)}) collective-permute-start(bf16[192,768]{1,0:T(8,128)(2,1)S(1)} %get-tuple-element.39), channel_id=1, source_target_pairs={{0,193},{64,0},{128,64},{192,128},{1,192},{65,1},{129,65},{193,129... | collective-permute-start | bytes 884744 | tf_op jit(solution)/shard_map/ppermute | solution.py:21
  42.7 16.4 %collective-permute-start.5 = (bf16[192,768]{1,0:T(8,128)(2,1)S(1)}, bf16[192,768]{1,0:T(8,128)(2,1)S(1)}, u32[]{:S(2)}, u32[]{:S(2)}) collective-permute-start(bf16[192,768]{1,0:T(8,128)(2,1)S(1)} %get-tuple-element.40), channel_id=1, source_target_pairs={{0,64},{64,128},{128,192},{192,1},{1,65},{65,129},{129,193},{193,0... | collective-permute-start | bytes 884744 | tf_op jit(solution)/shard_map/ppermute | solution.py:21
  59.0 35.8 %collective-permute-start.3 = (bf16[4,384,384]{2,1,0:T(8,128)(2,1)S(1)}, bf16[4,384,384]{2,1,0:T(8,128)(2,1)S(1)}, u32[]{:S(2)}, u32[]{:S(2)}) collective-permute-start(bf16[4,384,384]{2,1,0:T(8,128)(2,1)S(1)} %shard_map.56.mine), channel_id=1, source_target_pairs={{0,2},{2,0},{1,3},{3,1},{4,6},{6,4},{5,7},{7,5},{8,10},{10,8},{9,1... | collective-permute-start | bytes 3538952 | tf_op jit(solution)/shard_map/ppermute | solution.py:37
  71.1 23.1 %collective-permute-start.12 = (bf16[2,192,768]{2,1,0:T(8,128)(2,1)S(1)}, bf16[2,192,768]{2,1,0:T(8,128)(2,1)S(1)}, u32[]{:S(2)}, u32[]{:S(2)}) collective-permute-start(bf16[2,192,768]{2,1,0:T(8,128)(2,1)S(1)} %shard_map.59.refs_1_), channel_id=1, source_target_pairs={{0,48},{16,32},{32,16},{48,0},{1,49},{17,33},{33,17},{49,1},{2,50}... | collective-permute-start | bytes 1769480 | tf_op jit(solution)/shard_map/ppermute | solution.py:29
  71.5 39.1 %collective-permute-start.18 = (bf16[4,384,384]{2,1,0:T(8,128)(2,1)S(1)}, bf16[4,384,384]{2,1,0:T(8,128)(2,1)S(1)}, u32[]{:S(2)}, u32[]{:S(2)}) collective-permute-start(bf16[4,384,384]{2,1,0:T(8,128)(2,1)S(1)} %shard_map.62.mine), channel_id=1, source_target_pairs={{0,2},{2,0},{1,3},{3,1},{4,6},{6,4},{5,7},{7,5},{8,10},{10,8},{9,1... | collective-permute-start | bytes 3538952 | tf_op jit(solution)/shard_map/ppermute | solution.py:37
  78.2 13.8 %collective-permute-start.13 = (bf16[192,768]{1,0:T(8,128)(2,1)S(1)}, bf16[192,768]{1,0:T(8,128)(2,1)S(1)}, u32[]{:S(2)}, u32[]{:S(2)}) collective-permute-start(bf16[192,768]{1,0:T(8,128)(2,1)S(1)} %shard_map.60.refs_2_), channel_id=1, source_target_pairs={{0,48},{16,32},{32,16},{48,0},{1,49},{17,33},{33,17},{49,1},{2,50}... | collective-permute-start | bytes 884744 | tf_op jit(solution)/shard_map/ppermute | solution.py:29
  92.1 16.2 %collective-permute-start.9 = (bf16[2,192,768]{2,1,0:T(8,128)(2,1)S(1)}, bf16[2,192,768]{2,1,0:T(8,128)(2,1)S(1)}, u32[]{:S(2)}, u32[]{:S(2)}) collective-permute-start(bf16[2,192,768]{2,1,0:T(8,128)(2,1)S(1)} %shard_map.59.refs_1_), channel_id=1, source_target_pairs={{0,16},{16,0},{32,48},{48,32},{1,17},{17,1},{33,49},{49,33},{2,18}... | collective-permute-start | bytes 1769480 | tf_op jit(solution)/shard_map/ppermute | solution.py:29
  94.2 18.2 %collective-permute-start.19 = (bf16[2,192,768]{2,1,0:T(8,128)(2,1)S(1)}, bf16[2,192,768]{2,1,0:T(8,128)(2,1)S(1)}, u32[]{:S(2)}, u32[]{:S(2)}) collective-permute-start(bf16[2,192,768]{2,1,0:T(8,128)(2,1)S(1)} %shard_map.64), channel_id=1, source_target_pairs={{0,48},{16,32},{32,16},{48,0},{1,49},{17,33},{33,17},{49,1},{2,50}... | collective-permute-start | bytes 1769480 | tf_op jit(solution)/shard_map/ppermute | solution.py:29
  94.8 24.0 %collective-permute-start.20 = (bf16[2,192,768]{2,1,0:T(8,128)(2,1)S(1)}, bf16[2,192,768]{2,1,0:T(8,128)(2,1)S(1)}, u32[]{:S(2)}, u32[]{:S(2)}) collective-permute-start(bf16[2,192,768]{2,1,0:T(8,128)(2,1)S(1)} %collective-permute-done.12.refs_7_), channel_id=1, source_target_pairs={{0,16},{16,0},{32,48},{48,32},{1,17},{17,1},{33,49},{49,33},{2,18}... | collective-permute-start | bytes 1769480 | tf_op jit(solution)/shard_map/ppermute | solution.py:29
  131.8 16.3 %collective-permute-start.26 = (bf16[2,4,48,768]{3,2,1,0:T(8,128)(2,1)S(1)}, bf16[2,4,48,768]{3,2,1,0:T(8,128)(2,1)S(1)}, u32[]{:S(2)}, u32[]{:S(2)}) collective-permute-start(bf16[2,4,48,768]{3,2,1,0:T(8,128)(2,1)S(1)} %get-tuple-element.45), channel_id=1, source_target_pairs={{0,16},{16,0},{32,48},{48,32},{1,17},{17,1},{33,49},{49,33},{2,18}... | collective-permute-start | bytes 1769480 | tf_op jit(solution)/shard_map/ppermute | solution.py:29
  132.8 17.0 %collective-permute-start.30 = (bf16[2,4,48,768]{3,2,1,0:T(8,128)(2,1)S(1)}, bf16[2,4,48,768]{3,2,1,0:T(8,128)(2,1)S(1)}, u32[]{:S(2)}, u32[]{:S(2)}) collective-permute-start(bf16[2,4,48,768]{3,2,1,0:T(8,128)(2,1)S(1)} %get-tuple-element.51), channel_id=1, source_target_pairs={{0,48},{16,32},{32,16},{48,0},{1,49},{17,33},{33,17},{49,1},{2,50}... | collective-permute-start | bytes 1769480 | tf_op jit(solution)/shard_map/ppermute | solution.py:29
  137.2 16.5 %collective-permute-start.29 = (bf16[4,48,768]{2,1,0:T(8,128)(2,1)S(1)}, bf16[4,48,768]{2,1,0:T(8,128)(2,1)S(1)}, u32[]{:S(2)}, u32[]{:S(2)}) collective-permute-start(bf16[4,48,768]{2,1,0:T(8,128)(2,1)S(1)} %get-tuple-element.50), channel_id=1, source_target_pairs={{0,48},{16,32},{32,16},{48,0},{1,49},{17,33},{33,17},{49,1},{2,50}... | collective-permute-start | bytes 884744 | tf_op jit(solution)/shard_map/ppermute | solution.py:29
  137.5 16.2 %collective-permute-start.31 = (bf16[4,48,768]{2,1,0:T(8,128)(2,1)S(1)}, bf16[4,48,768]{2,1,0:T(8,128)(2,1)S(1)}, u32[]{:S(2)}, u32[]{:S(2)}) collective-permute-start(bf16[4,48,768]{2,1,0:T(8,128)(2,1)S(1)} %get-tuple-element.52), channel_id=1, source_target_pairs={{0,16},{16,0},{32,48},{48,32},{1,17},{17,1},{33,49},{49,33},{2,18}... | collective-permute-start | bytes 884744 | tf_op jit(solution)/shard_map/ppermute | solution.py:29
  156.9 21.7 %collective-permute-start.36 = (bf16[4,48,768]{2,1,0:T(8,128)(2,1)S(1)}, bf16[4,48,768]{2,1,0:T(8,128)(2,1)S(1)}, u32[]{:S(2)}, u32[]{:S(2)}) collective-permute-start(bf16[4,48,768]{2,1,0:T(8,128)(2,1)S(1)} %get-tuple-element.59), channel_id=1, source_target_pairs={{0,16},{16,0},{32,48},{48,32},{1,17},{17,1},{33,49},{49,33},{2,18}... | collective-permute-start | bytes 884744 | tf_op jit(solution)/shard_map/ppermute | solution.py:29
  158.5 20.1 %collective-permute-start.38 = (bf16[4,48,768]{2,1,0:T(8,128)(2,1)S(1)}, bf16[4,48,768]{2,1,0:T(8,128)(2,1)S(1)}, u32[]{:S(2)}, u32[]{:S(2)}) collective-permute-start(bf16[4,48,768]{2,1,0:T(8,128)(2,1)S(1)} %get-tuple-element.61), channel_id=1, source_target_pairs={{0,48},{16,32},{32,16},{48,0},{1,49},{17,33},{33,17},{49,1},{2,50}... | collective-permute-start | bytes 884744 | tf_op jit(solution)/shard_map/ppermute | solution.py:29
  159.1 19.5 %collective-permute-start.37 = (bf16[4,48,768]{2,1,0:T(8,128)(2,1)S(1)}, bf16[4,48,768]{2,1,0:T(8,128)(2,1)S(1)}, u32[]{:S(2)}, u32[]{:S(2)}) collective-permute-start(bf16[4,48,768]{2,1,0:T(8,128)(2,1)S(1)} %get-tuple-element.60), channel_id=1, source_target_pairs={{0,48},{16,32},{32,16},{48,0},{1,49},{17,33},{33,17},{49,1},{2,50}... | collective-permute-start | bytes 884744 | tf_op jit(solution)/shard_map/ppermute | solution.py:29
  160.7 17.9 %collective-permute-start.39 = (bf16[4,48,768]{2,1,0:T(8,128)(2,1)S(1)}, bf16[4,48,768]{2,1,0:T(8,128)(2,1)S(1)}, u32[]{:S(2)}, u32[]{:S(2)}) collective-permute-start(bf16[4,48,768]{2,1,0:T(8,128)(2,1)S(1)} %get-tuple-element.62), channel_id=1, source_target_pairs={{0,16},{16,0},{32,48},{48,32},{1,17},{17,1},{33,49},{49,33},{2,18}... | collective-permute-start | bytes 884744 | tf_op jit(solution)/shard_map/ppermute | solution.py:29
  179.0 14.5 %collective-permute-start.41 = (bf16[96,384]{1,0:T(8,128)(2,1)S(1)}, bf16[96,384]{1,0:T(8,128)(2,1)S(1)}, u32[]{:S(2)}, u32[]{:S(2)}) collective-permute-start(bf16[96,384]{1,0:T(8,128)(2,1)S(1)} %get-tuple-element.65), channel_id=1, source_target_pairs={{0,128},{64,192},{128,1},{192,65},{1,129},{65,193},{129,0},{193,64... | collective-permute-start | bytes 221192 | tf_op jit(solution)/shard_map/ppermute | solution.py:21
  (27 other events, 312.2 us)
where the time goes:
time: 200 us
  waiting for transfers between devices  104 us (52%)
  starting transfers between devices  69.1 us (35%)
  Pallas kernels  25.1 us (13%)
    ppermute x18, waiting for transfers between devices, flip_x(): return lax.ppermute(v, 'x', [(i, i ^ j) for i in range(4)])  49.9 us
    ppermute x13, starting transfers between devices, shift_z(): lax.ppermute(v, ('zl', 'zh'), [(_zi(z), _zi((z + k) % 8)) for z in range(...  35.7 us
    pallas_call x22, Pallas kernels, call(): pl.pallas_call(body, out_shape=outs, in_specs=[pl.BlockSpec(memory_space=...  25.1 us
    ppermute x10, waiting for transfers between devices, shift_y(): return lax.ppermute(v, 'y', [(i, (i + k) % 4) for i in range(4)])  23.1 us
    ppermute x13, waiting for transfers between devices, shift_z(): lax.ppermute(v, ('zl', 'zh'), [(_zi(z), _zi((z + k) % 8)) for z in range(...  21.6 us
    ppermute x18, starting transfers between devices, flip_x(): return lax.ppermute(v, 'x', [(i, i ^ j) for i in range(4)])  17.8 us
    ppermute x10, starting transfers between devices, shift_y(): return lax.ppermute(v, 'y', [(i, (i + k) % 4) for i in range(4)])  12 us
    ppermute x3, waiting for transfers between devices, flip_z(): return lax.ppermute(v, 'zl', [(i, i ^ j) for i in range(4)])  9.52 us
  transfers between devices with their start and end apart: 47, of which 20 were waited for; matrix products, arithmetic and copies ran while one was open for 0% of the time, Pallas kernels for 11%

commit v1 on v0

--- a/solution.py
+++ b/solution.py
@@ -140,17 +140,15 @@
     parity, same = x % 2, (x // 2) == core
 
     def run(par, sm):
-        def step(n, _):
-            r = n // 4
+        def step(r, _):
             ry = (zl + r - y + 4) % 4
-            part = pl.ds(pl.multiple_of((n % 4) * 96, 96), 96)
             for j in range(4):
                 src = mine if ((j < 2) == sm) else other
                 start = ((par + j) % 2) * 192
-                out[j, r, part] = src[ry, part, start : start + 192]
+                out[j, r] = src[ry, :, start : start + 192]
             return 0
 
-        lax.fori_loop(0, 16, step, 0)
+        lax.fori_loop(0, 4, step, 0)
 
     for par in range(2):
         for sm in range(2):
@@ -319,26 +317,29 @@
     out[:96], out[96:] = a[...], b[...]
 
 
-def zprep0_body(o0, m1, t3, m3, t1, *outs):
+def zprep0_body(o0, m1, t3, m3, t1, own, far, pair):
     zl0 = place()[0]
-    for k in range(4):
+    for k, out in enumerate((own, pair.at[0], far, pair.at[1])):
         zl = zl0 ^ k
         for q, (u, v) in enumerate(((m1.at[0], t3), (m3.at[0], t1))):
-            own = o0[zl, q * 48 : (q + 1) * 48]
-            outs[k][48 * q : 48 * (q + 1)] = (
-                own.astype(F32) + u[zl].astype(F32) + v[zl].astype(F32)
+            o = o0[zl, q * 48 : (q + 1) * 48]
+            out[48 * q : 48 * (q + 1)] = (
+                o.astype(F32) + u[zl].astype(F32) + v[zl].astype(F32)
             ).astype(BF16)
 
 
-def zsum_body(a, b, c, d, keep, give):
+def zmid_body(own, far, pair, a, b):
+    a[...] = own[...].astype(F32) + pair[0].astype(F32)
+    b[...] = (far[...].astype(F32) + pair[1].astype(F32)).astype(BF16)
+
+
+def zsum_body(a, b, keep, give):
     zh = place()[4]
 
     def run(half):
         for h in range(2):
             cols = slice(h * 384, (h + 1) * 384)
-            total = a[:, cols].astype(F32)
-            for r in (b, c, d):
-                total = total + r[:, cols].astype(F32)
+            total = a[:, cols] + b[:, cols].astype(F32)
             if h == half:
                 keep[...] = total
             else:
@@ -490,11 +491,20 @@
     t3[1] = flip_x(ta, 3)
     t1[1] = flip_x(tb, 1)
     (o0,) = call(term0_body, [sds(4, 192, 768)], args, mib=16, flops=1 << 30, nbytes=6 << 20)
-    got = call(zprep0_body, [sds(96, 768)] * 4, [o0, m1, t3[0], m3, t1[0]], nbytes=4 << 20)
-    got = [got[0]] + [flip_z(got[k], k) for k in (1, 2, 3)]
+    own, fard, pairs = call(
+        zprep0_body,
+        [sds(96, 768), sds(96, 768), sds(2, 96, 768)],
+        [o0, m1, t3[0], m3, t1[0]],
+        nbytes=4 << 20,
+    )
+    pairs = flip_z(pairs, 1)
+    a, b = call(
+        zmid_body, [sds(96, 768, dtype=F32), sds(96, 768)], [own, fard, pairs], nbytes=1 << 20
+    )
+    b = flip_z(b, 2)
     last = call(zlast_body, [sds(96, 384)] * 8, [o0, s1b, t3[1], s3b, t1[1]], nbytes=4 << 20)
     last = [last[0]] + [shift_z(last[k], k) for k in range(1, 8)]
-    keep, give = call(zsum_body, [sds(96, 384, dtype=F32), sds(96, 384)], got, nbytes=1 << 20)
+    keep, give = call(zsum_body, [sds(96, 384, dtype=F32), sds(96, 384)], [a, b], nbytes=1 << 20)
     give = shift_z(give, 4)
     return call(final_body, sds(2, 192, 384), [keep, give, *last], nbytes=2 << 20)
 

time: 200 us -> 198 us (0.990)
  the two profiles are of different devices: /device:TPU:4 before, /device:TPU:54 now
where the time goes in v1:
time: 198 us
  waiting for transfers between devices  109 us (55%)
  starting transfers between devices  64.3 us (32%)
  Pallas kernels  23 us (12%)
    ppermute x18, waiting for transfers between devices, flip_x(): return lax.ppermute(v, 'x', [(i, i ^ j) for i in range(4)])  60.4 us
    ppermute x13, starting transfers between devices, shift_z(): lax.ppermute(v, ('zl', 'zh'), [(_zi(z), _zi((z + k) % 8)) for z in range(...  32.5 us
    ppermute x13, waiting for transfers between devices, shift_z(): lax.ppermute(v, ('zl', 'zh'), [(_zi(z), _zi((z + k) % 8)) for z in range(...  24.4 us
    pallas_call x23, Pallas kernels, call(): pl.pallas_call(body, out_shape=outs, in_specs=[pl.BlockSpec(memory_space=...  23 us
    ppermute x10, waiting for transfers between devices, shift_y(): return lax.ppermute(v, 'y', [(i, (i + k) % 4) for i in range(4)])  21.1 us
    ppermute x18, starting transfers between devices, flip_x(): return lax.ppermute(v, 'x', [(i, i ^ j) for i in range(4)])  17.1 us
    ppermute x10, starting transfers between devices, shift_y(): return lax.ppermute(v, 'y', [(i, (i + k) % 4) for i in range(4)])  14.4 us
  transfers between devices with their start and end apart: 46, of which 26 were waited for; matrix products, arithmetic and copies ran while one was open for 0% of the time, Pallas kernels for 10%

profile of v1, /device:TPU:54, one launch (start us, length us, event | category | flops | bytes accessed | tf_op | source)
XLA Modules:
  0.0 198.3 jit_solution(14079573839498792789)
XLA Ops:
  3.5 13.0 %collective-permute-done.21.a.s1 = bf16[384,768]{1,0:T(8,128)(2,1)S(1)} collective-permute-done((bf16[384,768]{1,0:T(8,128)(2,1)S(1)}, bf16[384,768]{1,0:T(8,128)(2,1)S(1)}, u32[]{:S(2)}, u32[]{:S(2)}) %collective-permute-start.21) | collective-permute-done | bytes 589856 | tf_op jit(solution)/shard_map/ppermute | solution.py:25
  21.8 3.3 %collective-permute-start.6 = (bf16[96,768]{1,0:T(8,128)(2,1)S(1)}, bf16[96,768]{1,0:T(8,128)(2,1)S(1)}, u32[]{:S(2)}, u32[]{:S(2)}) collective-permute-start(bf16[96,768]{1,0:T(8,128)(2,1)S(1)} %get-tuple-element.42), channel_id=1, source_target_pairs={{0,128},{64,192},{128,1},{192,65},{1,129},{65,193},{129,0},{193,64... | collective-permute-start | bytes 442376 | tf_op jit(solution)/shard_map/ppermute | solution.py:21
  27.4 3.4 %collective-permute-start.1 = (bf16[384,384]{1,0:T(8,128)(2,1)S(1)}, bf16[384,384]{1,0:T(8,128)(2,1)S(1)}, u32[]{:S(2)}, u32[]{:S(2)}) collective-permute-start(bf16[384,384]{1,0:T(8,128)(2,1)S(1)} %bitcast.14), channel_id=1, source_target_pairs={{0,8},{4,12},{8,0},{12,4},{1,9},{5,13},{9,1},{13,5},{2,10},{6,14},... | collective-permute-start | bytes 884744 | tf_op jit(solution)/shard_map/ppermute | solution.py:25
  32.6 4.9 %collective-permute-start.14 = (bf16[384,384]{1,0:T(8,128)(2,1)S(1)}, bf16[384,384]{1,0:T(8,128)(2,1)S(1)}, u32[]{:S(2)}, u32[]{:S(2)}) collective-permute-start(bf16[384,384]{1,0:T(8,128)(2,1)S(1)} %bitcast.15), channel_id=1, source_target_pairs={{0,1},{64,65},{128,129},{192,193},{1,0},{65,64},{129,128},{193,192... | collective-permute-start | bytes 884744 | tf_op jit(solution)/shard_map/ppermute | solution.py:21
  39.7 13.1 %collective-permute-done.14.refs_0_ = bf16[384,384]{1,0:T(8,128)(2,1)S(1)} collective-permute-done((bf16[384,384]{1,0:T(8,128)(2,1)S(1)}, bf16[384,384]{1,0:T(8,128)(2,1)S(1)}, u32[]{:S(2)}, u32[]{:S(2)}) %collective-permute-start.14) | collective-permute-done | bytes 294944 | tf_op jit(solution)/shard_map/ppermute | solution.py:21
  58.7 3.9 %collective-permute-done.15.refs_1_ = bf16[384,384]{1,0:T(8,128)(2,1)S(1)} collective-permute-done((bf16[384,384]{1,0:T(8,128)(2,1)S(1)}, bf16[384,384]{1,0:T(8,128)(2,1)S(1)}, u32[]{:S(2)}, u32[]{:S(2)}) %collective-permute-start.15) | collective-permute-done | bytes 294944 | tf_op jit(solution)/shard_map/ppermute | solution.py:25
  64.6 4.0 %collective-permute-done.17.refs_3_ = bf16[384,384]{1,0:T(8,128)(2,1)S(1)} collective-permute-done((bf16[384,384]{1,0:T(8,128)(2,1)S(1)}, bf16[384,384]{1,0:T(8,128)(2,1)S(1)}, u32[]{:S(2)}, u32[]{:S(2)}) %collective-permute-start.17) | collective-permute-done | bytes 294944 | tf_op jit(solution)/shard_map/ppermute | solution.py:25
  71.3 6.1 %collective-permute-done.10.refs_5_.refs_1_ = bf16[192,768]{1,0:T(8,128)(2,1)S(1)} collective-permute-done((bf16[192,768]{1,0:T(8,128)(2,1)S(1)}, bf16[192,768]{1,0:T(8,128)(2,1)S(1)}, u32[]{:S(2)}, u32[]{:S(2)}) %collective-permute-start.10) | collective-permute-done | bytes 294944 | tf_op jit(solution)/shard_map/ppermute | solution.py:29
  77.9 14.2 %collective-permute-done.13.refs_8_ = bf16[192,768]{1,0:T(8,128)(2,1)S(1)} collective-permute-done((bf16[192,768]{1,0:T(8,128)(2,1)S(1)}, bf16[192,768]{1,0:T(8,128)(2,1)S(1)}, u32[]{:S(2)}, u32[]{:S(2)}) %collective-permute-start.13) | collective-permute-done | bytes 294944 | tf_op jit(solution)/shard_map/ppermute | solution.py:29
  94.9 4.3 %shard_map.55.coef = f32[384,128]{1,0:T(8,128)S(1)} custom-call(f32[4,4,12]{2,1,0:T(4,128)S(1)} %bitcast.18, s32[12]{0:T(128)S(1)} %copy-done.2, s32[12]{0:T(128)S(1)} %copy-done.3), custom_call_target="tpu_custom_call" | custom-call | bytes 1048576 | tf_op jit(solution)/shard_map/pallas_call | solution.py:42
  99.9 8.5 %collective-permute-done.9.refs_4_ = bf16[2,192,768]{2,1,0:T(8,128)(2,1)S(1)} collective-permute-done((bf16[2,192,768]{2,1,0:T(8,128)(2,1)S(1)}, bf16[2,192,768]{2,1,0:T(8,128)(2,1)S(1)}, u32[]{:S(2)}, u32[]{:S(2)}) %collective-permute-start.9) | collective-permute-done | bytes 589856 | tf_op jit(solution)/shard_map/ppermute | solution.py:29
  108.3 2.3 %shard_map.61.part = f32[384,768]{1,0:T(8,128)S(1)} custom-call(bf16[4,4,384,192]{3,2,1,0:T(8,128)(2,1)S(1)} %shard_map.57.e.e0, bf16[192,768]{1,0:T(8,128)(2,1)S(1)} %get-tuple-element.39.refs_0_, bf16[2,192,768]{2,1,0:T(8,128)(2,1)S(1)} %shard_map.59.refs_1_, bf16[192,768]{1,0:T(8,128)(2,1)S(1)} %shard_map.60.refs_2_, ...), custom_call_target="tpu_custom_call" | custom-call | flops 1358954496 | bytes 8388608 | tf_op jit(solution)/shard_map/pallas_call | solution.py:42
  111.4 7.5 %collective-permute-done.20.refs_10_ = bf16[2,192,768]{2,1,0:T(8,128)(2,1)S(1)} collective-permute-done((bf16[2,192,768]{2,1,0:T(8,128)(2,1)S(1)}, bf16[2,192,768]{2,1,0:T(8,128)(2,1)S(1)}, u32[]{:S(2)}, u32[]{:S(2)}) %collective-permute-start.20) | collective-permute-done | bytes 589856 | tf_op jit(solution)/shard_map/ppermute | solution.py:29
  118.9 6.1 %shard_map.65.m_ref = bf16[768,768]{1,0:T(8,128)(2,1)S(1)} custom-call(f32[384,128]{1,0:T(8,128)S(1)} %shard_map.55.coef, f32[384,768]{1,0:T(8,128)S(1)} %shard_map.61.part, bf16[4,4,384,192]{3,2,1,0:T(8,128)(2,1)S(1)} %shard_map.57.e.e0, bf16[4,4,384,192]{3,2,1,0:T(8,128)(2,1)S(1)} %shard_map.63.e1, bf16[192,768]{1,0:T(8,128)(2,1)S(1)} %get-tuple-element.39.refs_0_, ...), custom_call_target="tpu_custom_call" | custom-call | flops 2264924160 | bytes 12582912 | tf_op jit(solution)/shard_map/pallas_call | solution.py:42
  127.8 3.2 %shard_map.69 = (bf16[2,4,48,768]{3,2,1,0:T(8,128)(2,1)S(1)}, bf16[2,4,48,768]{3,2,1,0:T(8,128)(2,1)S(1)}, bf16[4,48,768]{2,1,0:T(8,128)(2,1)S(1)}, bf16[4,48,76...) custom-call(bf16[768,768]{1,0:T(8,128)(2,1)S(1)} %shard_map.65.m_ref, ...), custom_call_target="tpu_custom_call" | custom-call | flops 2147483648 | bytes 8388608 | tf_op jit(solution)/shard_map/pallas_call | solution.py:42
  139.1 8.8 %collective-permute-done.26.m1.ra = bf16[2,4,48,768]{3,2,1,0:T(8,128)(2,1)S(1)} collective-permute-done((bf16[2,4,48,768]{3,2,1,0:T(8,128)(2,1)S(1)}, bf16[2,4,48,768]{3,2,1,0:T(8,128)(2,1)S(1)}, u32[]{:S(2)}, u32[]{:S(2)}) %collective-permute-start.26) | collective-permute-done | bytes 589856 | tf_op jit(solution)/shard_map/ppermute | solution.py:29
  149.7 4.1 %collective-permute-done.29.t3 = bf16[4,48,768]{2,1,0:T(8,128)(2,1)S(1)} collective-permute-done((bf16[4,48,768]{2,1,0:T(8,128)(2,1)S(1)}, bf16[4,48,768]{2,1,0:T(8,128)(2,1)S(1)}, u32[]{:S(2)}, u32[]{:S(2)}) %collective-permute-start.29) | collective-permute-done | bytes 294944 | tf_op jit(solution)/shard_map/ppermute | solution.py:29
  158.5 3.4 %collective-permute-done.32.pair = bf16[2,96,768]{2,1,0:T(8,128)(2,1)S(1)} collective-permute-done((bf16[2,96,768]{2,1,0:T(8,128)(2,1)S(1)}, bf16[2,96,768]{2,1,0:T(8,128)(2,1)S(1)}, u32[]{:S(2)}, u32[]{:S(2)}) %collective-permute-start.32) | collective-permute-done | bytes 294944 | tf_op jit(solution)/shard_map/ppermute | solution.py:33
  165.6 3.2 %collective-permute-done.36.t3 = bf16[4,48,768]{2,1,0:T(8,128)(2,1)S(1)} collective-permute-done((bf16[4,48,768]{2,1,0:T(8,128)(2,1)S(1)}, bf16[4,48,768]{2,1,0:T(8,128)(2,1)S(1)}, u32[]{:S(2)}, u32[]{:S(2)}) %collective-permute-start.36) | collective-permute-done | bytes 294944 | tf_op jit(solution)/shard_map/ppermute | solution.py:29
  169.6 6.8 %collective-permute-start.40 = (bf16[96,384]{1,0:T(8,128)(2,1)S(1)}, bf16[96,384]{1,0:T(8,128)(2,1)S(1)}, u32[]{:S(2)}, u32[]{:S(2)}) collective-permute-start(bf16[96,384]{1,0:T(8,128)(2,1)S(1)} %get-tuple-element.67), channel_id=1, source_target_pairs={{0,128},{64,192},{128,1},{192,65},{1,129},{65,193},{129,0},{193,64... | collective-permute-start | bytes 221192 | tf_op jit(solution)/shard_map/ppermute | solution.py:21
  177.1 4.4 %collective-permute-start.43 = (bf16[96,384]{1,0:T(8,128)(2,1)S(1)}, bf16[96,384]{1,0:T(8,128)(2,1)S(1)}, u32[]{:S(2)}, u32[]{:S(2)}) collective-permute-start(bf16[96,384]{1,0:T(8,128)(2,1)S(1)} %get-tuple-element.70), channel_id=1, source_target_pairs={{0,65},{64,129},{128,193},{192,0},{1,64},{65,128},{129,192},{193,1... | collective-permute-start | bytes 221192 | tf_op jit(solution)/shard_map/ppermute | solution.py:21
  183.9 3.1 %collective-permute-start.45 = (bf16[96,384]{1,0:T(8,128)(2,1)S(1)}, bf16[96,384]{1,0:T(8,128)(2,1)S(1)}, u32[]{:S(2)}, u32[]{:S(2)}) collective-permute-start(bf16[96,384]{1,0:T(8,128)(2,1)S(1)} %get-tuple-element.72), channel_id=1, source_target_pairs={{0,193},{64,0},{128,64},{192,128},{1,192},{65,1},{129,65},{193,129... | collective-permute-start | bytes 221192 | tf_op jit(solution)/shard_map/ppermute | solution.py:21
  189.6 2.5 %collective-permute-done.44.refs_6_ = bf16[96,384]{1,0:T(8,128)(2,1)S(1)} collective-permute-done((bf16[96,384]{1,0:T(8,128)(2,1)S(1)}, bf16[96,384]{1,0:T(8,128)(2,1)S(1)}, u32[]{:S(2)}, u32[]{:S(2)}) %collective-permute-start.44) | collective-permute-done | bytes 73760 | tf_op jit(solution)/shard_map/ppermute | solution.py:21
  193.6 3.5 %collective-permute-done.34.give = bf16[96,384]{1,0:T(8,128)(2,1)S(1)} collective-permute-done((bf16[96,384]{1,0:T(8,128)(2,1)S(1)}, bf16[96,384]{1,0:T(8,128)(2,1)S(1)}, u32[]{:S(2)}, u32[]{:S(2)}) %collective-permute-start.34) | collective-permute-done | bytes 73760 | tf_op jit(solution)/shard_map/ppermute | solution.py:21
  (101 shorter events, 60.3 us)
Async XLA Ops:
  1.4 15.1 %collective-permute-start.21 = (bf16[384,768]{1,0:T(8,128)(2,1)S(1)}, bf16[384,768]{1,0:T(8,128)(2,1)S(1)}, u32[]{:S(2)}, u32[]{:S(2)}) collective-permute-start(bf16[384,768]{1,0:T(8,128)(2,1)S(1)} %bitcast.7), channel_id=1, source_target_pairs={{0,12},{4,0},{8,4},{12,8},{1,13},{5,1},{9,5},{13,9},{2,14},{6,2},{... | collective-permute-start | bytes 1769480 | tf_op jit(solution)/shard_map/ppermute | solution.py:25
  1.9 14.8 %collective-permute-start.22 = (bf16[384,768]{1,0:T(8,128)(2,1)S(1)}, bf16[384,768]{1,0:T(8,128)(2,1)S(1)}, u32[]{:S(2)}, u32[]{:S(2)}) collective-permute-start(bf16[384,768]{1,0:T(8,128)(2,1)S(1)} %bitcast.8), channel_id=1, source_target_pairs={{0,4},{4,8},{8,12},{12,0},{1,5},{5,9},{9,13},{13,1},{2,6},{6,10},{... | collective-permute-start | bytes 1769480 | tf_op jit(solution)/shard_map/ppermute | solution.py:25
  19.3 18.4 %collective-permute-start = (bf16[384,384]{1,0:T(8,128)(2,1)S(1)}, bf16[384,384]{1,0:T(8,128)(2,1)S(1)}, u32[]{:S(2)}, u32[]{:S(2)}) collective-permute-start(bf16[384,384]{1,0:T(8,128)(2,1)S(1)} %bitcast.13), channel_id=1, source_target_pairs={{0,12},{4,0},{8,4},{12,8},{1,13},{5,1},{9,5},{13,9},{2,14},{6,2},{... | collective-permute-start | bytes 884744 | tf_op jit(solution)/shard_map/ppermute | solution.py:25
  31.0 94.0 %collective-permute-start.25 = (bf16[4,384,768]{2,1,0:T(8,128)(2,1)S(1)}, bf16[4,384,768]{2,1,0:T(8,128)(2,1)S(1)}, u32[]{:S(2)}, u32[]{:S(2)}) collective-permute-start(bf16[4,384,768]{2,1,0:T(8,128)(2,1)S(1)} %shard_map.67.mine), channel_id=1, source_target_pairs={{0,2},{2,0},{1,3},{3,1},{4,6},{6,4},{5,7},{7,5},{8,10},{10,8},{9,1... | collective-permute-start | bytes 7077896 | tf_op jit(solution)/shard_map/ppermute | solution.py:37
  32.6 20.2 %collective-permute-start.14 = (bf16[384,384]{1,0:T(8,128)(2,1)S(1)}, bf16[384,384]{1,0:T(8,128)(2,1)S(1)}, u32[]{:S(2)}, u32[]{:S(2)}) collective-permute-start(bf16[384,384]{1,0:T(8,128)(2,1)S(1)} %bitcast.15), channel_id=1, source_target_pairs={{0,1},{64,65},{128,129},{192,193},{1,0},{65,64},{129,128},{193,192... | collective-permute-start | bytes 884744 | tf_op jit(solution)/shard_map/ppermute | solution.py:21
  37.5 16.5 %collective-permute-start.2 = (bf16[384,384]{1,0:T(8,128)(2,1)S(1)}, bf16[384,384]{1,0:T(8,128)(2,1)S(1)}, u32[]{:S(2)}, u32[]{:S(2)}) collective-permute-start(bf16[384,384]{1,0:T(8,128)(2,1)S(1)} %bitcast.16), channel_id=1, source_target_pairs={{0,4},{4,8},{8,12},{12,0},{1,5},{5,9},{9,13},{13,1},{2,6},{6,10},{... | collective-permute-start | bytes 884744 | tf_op jit(solution)/shard_map/ppermute | solution.py:25
  37.6 20.1 %collective-permute-start.4 = (bf16[192,768]{1,0:T(8,128)(2,1)S(1)}, bf16[192,768]{1,0:T(8,128)(2,1)S(1)}, u32[]{:S(2)}, u32[]{:S(2)}) collective-permute-start(bf16[192,768]{1,0:T(8,128)(2,1)S(1)} %get-tuple-element.40), channel_id=1, source_target_pairs={{0,193},{64,0},{128,64},{192,128},{1,192},{65,1},{129,65},{193,129... | collective-permute-start | bytes 884744 | tf_op jit(solution)/shard_map/ppermute | solution.py:21
  39.1 18.7 %collective-permute-start.5 = (bf16[192,768]{1,0:T(8,128)(2,1)S(1)}, bf16[192,768]{1,0:T(8,128)(2,1)S(1)}, u32[]{:S(2)}, u32[]{:S(2)}) collective-permute-start(bf16[192,768]{1,0:T(8,128)(2,1)S(1)} %get-tuple-element.41), channel_id=1, source_target_pairs={{0,64},{64,128},{128,192},{192,1},{1,65},{65,129},{129,193},{193,0... | collective-permute-start | bytes 884744 | tf_op jit(solution)/shard_map/ppermute | solution.py:21
  57.7 35.7 %collective-permute-start.3 = (bf16[4,384,384]{2,1,0:T(8,128)(2,1)S(1)}, bf16[4,384,384]{2,1,0:T(8,128)(2,1)S(1)}, u32[]{:S(2)}, u32[]{:S(2)}) collective-permute-start(bf16[4,384,384]{2,1,0:T(8,128)(2,1)S(1)} %shard_map.56.mine), channel_id=1, source_target_pairs={{0,2},{2,0},{1,3},{3,1},{4,6},{6,4},{5,7},{7,5},{8,10},{10,8},{9,1... | collective-permute-start | bytes 3538952 | tf_op jit(solution)/shard_map/ppermute | solution.py:37
  69.6 22.6 %collective-permute-start.12 = (bf16[2,192,768]{2,1,0:T(8,128)(2,1)S(1)}, bf16[2,192,768]{2,1,0:T(8,128)(2,1)S(1)}, u32[]{:S(2)}, u32[]{:S(2)}) collective-permute-start(bf16[2,192,768]{2,1,0:T(8,128)(2,1)S(1)} %shard_map.59.refs_1_), channel_id=1, source_target_pairs={{0,48},{16,32},{32,16},{48,0},{1,49},{17,33},{33,17},{49,1},{2,50}... | collective-permute-start | bytes 1769480 | tf_op jit(solution)/shard_map/ppermute | solution.py:29
  71.3 39.3 %collective-permute-start.18 = (bf16[4,384,384]{2,1,0:T(8,128)(2,1)S(1)}, bf16[4,384,384]{2,1,0:T(8,128)(2,1)S(1)}, u32[]{:S(2)}, u32[]{:S(2)}) collective-permute-start(bf16[4,384,384]{2,1,0:T(8,128)(2,1)S(1)} %shard_map.62.mine), channel_id=1, source_target_pairs={{0,2},{2,0},{1,3},{3,1},{4,6},{6,4},{5,7},{7,5},{8,10},{10,8},{9,1... | collective-permute-start | bytes 3538952 | tf_op jit(solution)/shard_map/ppermute | solution.py:37
  77.5 14.7 %collective-permute-start.13 = (bf16[192,768]{1,0:T(8,128)(2,1)S(1)}, bf16[192,768]{1,0:T(8,128)(2,1)S(1)}, u32[]{:S(2)}, u32[]{:S(2)}) collective-permute-start(bf16[192,768]{1,0:T(8,128)(2,1)S(1)} %shard_map.60.refs_2_), channel_id=1, source_target_pairs={{0,48},{16,32},{32,16},{48,0},{1,49},{17,33},{33,17},{49,1},{2,50}... | collective-permute-start | bytes 884744 | tf_op jit(solution)/shard_map/ppermute | solution.py:29
  92.1 16.2 %collective-permute-start.9 = (bf16[2,192,768]{2,1,0:T(8,128)(2,1)S(1)}, bf16[2,192,768]{2,1,0:T(8,128)(2,1)S(1)}, u32[]{:S(2)}, u32[]{:S(2)}) collective-permute-start(bf16[2,192,768]{2,1,0:T(8,128)(2,1)S(1)} %shard_map.59.refs_1_), channel_id=1, source_target_pairs={{0,16},{16,0},{32,48},{48,32},{1,17},{17,1},{33,49},{49,33},{2,18}... | collective-permute-start | bytes 1769480 | tf_op jit(solution)/shard_map/ppermute | solution.py:29
  92.2 19.2 %collective-permute-start.19 = (bf16[2,192,768]{2,1,0:T(8,128)(2,1)S(1)}, bf16[2,192,768]{2,1,0:T(8,128)(2,1)S(1)}, u32[]{:S(2)}, u32[]{:S(2)}) collective-permute-start(bf16[2,192,768]{2,1,0:T(8,128)(2,1)S(1)} %shard_map.64), channel_id=1, source_target_pairs={{0,48},{16,32},{32,16},{48,0},{1,49},{17,33},{33,17},{49,1},{2,50}... | collective-permute-start | bytes 1769480 | tf_op jit(solution)/shard_map/ppermute | solution.py:29
  93.4 25.5 %collective-permute-start.20 = (bf16[2,192,768]{2,1,0:T(8,128)(2,1)S(1)}, bf16[2,192,768]{2,1,0:T(8,128)(2,1)S(1)}, u32[]{:S(2)}, u32[]{:S(2)}) collective-permute-start(bf16[2,192,768]{2,1,0:T(8,128)(2,1)S(1)} %collective-permute-done.12.refs_7_), channel_id=1, source_target_pairs={{0,16},{16,0},{32,48},{48,32},{1,17},{17,1},{33,49},{49,33},{2,18}... | collective-permute-start | bytes 1769480 | tf_op jit(solution)/shard_map/ppermute | solution.py:29
  131.1 16.8 %collective-permute-start.26 = (bf16[2,4,48,768]{3,2,1,0:T(8,128)(2,1)S(1)}, bf16[2,4,48,768]{3,2,1,0:T(8,128)(2,1)S(1)}, u32[]{:S(2)}, u32[]{:S(2)}) collective-permute-start(bf16[2,4,48,768]{3,2,1,0:T(8,128)(2,1)S(1)} %get-tuple-element.46), channel_id=1, source_target_pairs={{0,16},{16,0},{32,48},{48,32},{1,17},{17,1},{33,49},{49,33},{2,18}... | collective-permute-start | bytes 1769480 | tf_op jit(solution)/shard_map/ppermute | solution.py:29
  132.3 17.4 %collective-permute-start.30 = (bf16[2,4,48,768]{3,2,1,0:T(8,128)(2,1)S(1)}, bf16[2,4,48,768]{3,2,1,0:T(8,128)(2,1)S(1)}, u32[]{:S(2)}, u32[]{:S(2)}) collective-permute-start(bf16[2,4,48,768]{3,2,1,0:T(8,128)(2,1)S(1)} %get-tuple-element.52), channel_id=1, source_target_pairs={{0,48},{16,32},{32,16},{48,0},{1,49},{17,33},{33,17},{49,1},{2,50}... | collective-permute-start | bytes 1769480 | tf_op jit(solution)/shard_map/ppermute | solution.py:29
  136.6 17.2 %collective-permute-start.29 = (bf16[4,48,768]{2,1,0:T(8,128)(2,1)S(1)}, bf16[4,48,768]{2,1,0:T(8,128)(2,1)S(1)}, u32[]{:S(2)}, u32[]{:S(2)}) collective-permute-start(bf16[4,48,768]{2,1,0:T(8,128)(2,1)S(1)} %get-tuple-element.51), channel_id=1, source_target_pairs={{0,48},{16,32},{32,16},{48,0},{1,49},{17,33},{33,17},{49,1},{2,50}... | collective-permute-start | bytes 884744 | tf_op jit(solution)/shard_map/ppermute | solution.py:29
  136.8 17.0 %collective-permute-start.31 = (bf16[4,48,768]{2,1,0:T(8,128)(2,1)S(1)}, bf16[4,48,768]{2,1,0:T(8,128)(2,1)S(1)}, u32[]{:S(2)}, u32[]{:S(2)}) collective-permute-start(bf16[4,48,768]{2,1,0:T(8,128)(2,1)S(1)} %get-tuple-element.53), channel_id=1, source_target_pairs={{0,16},{16,0},{32,48},{48,32},{1,17},{17,1},{33,49},{49,33},{2,18}... | collective-permute-start | bytes 884744 | tf_op jit(solution)/shard_map/ppermute | solution.py:29
  155.8 13.0 %collective-permute-start.36 = (bf16[4,48,768]{2,1,0:T(8,128)(2,1)S(1)}, bf16[4,48,768]{2,1,0:T(8,128)(2,1)S(1)}, u32[]{:S(2)}, u32[]{:S(2)}) collective-permute-start(bf16[4,48,768]{2,1,0:T(8,128)(2,1)S(1)} %get-tuple-element.62), channel_id=1, source_target_pairs={{0,48},{16,32},{32,16},{48,0},{1,49},{17,33},{33,17},{49,1},{2,50}... | collective-permute-start | bytes 884744 | tf_op jit(solution)/shard_map/ppermute | solution.py:29
  162.0 15.1 %collective-permute-start.33 = (bf16[96,768]{1,0:T(8,128)(2,1)S(1)}, bf16[96,768]{1,0:T(8,128)(2,1)S(1)}, u32[]{:S(2)}, u32[]{:S(2)}) collective-permute-start(bf16[96,768]{1,0:T(8,128)(2,1)S(1)} %get-tuple-element.58), channel_id=1, source_target_pairs={{0,128},{64,192},{128,0},{192,64},{1,129},{65,193},{129,1},{193,65... | collective-permute-start | bytes 442376 | tf_op jit(solution)/shard_map/ppermute | solution.py:33
  169.1 12.5 %collective-permute-start.39 = (bf16[96,384]{1,0:T(8,128)(2,1)S(1)}, bf16[96,384]{1,0:T(8,128)(2,1)S(1)}, u32[]{:S(2)}, u32[]{:S(2)}) collective-permute-start(bf16[96,384]{1,0:T(8,128)(2,1)S(1)} %get-tuple-element.66), channel_id=1, source_target_pairs={{0,64},{64,128},{128,192},{192,1},{1,65},{65,129},{129,193},{193,0... | collective-permute-start | bytes 221192 | tf_op jit(solution)/shard_map/ppermute | solution.py:21
  169.6 14.3 %collective-permute-start.40 = (bf16[96,384]{1,0:T(8,128)(2,1)S(1)}, bf16[96,384]{1,0:T(8,128)(2,1)S(1)}, u32[]{:S(2)}, u32[]{:S(2)}) collective-permute-start(bf16[96,384]{1,0:T(8,128)(2,1)S(1)} %get-tuple-element.67), channel_id=1, source_target_pairs={{0,128},{64,192},{128,1},{192,65},{1,129},{65,193},{129,0},{193,64... | collective-permute-start | bytes 221192 | tf_op jit(solution)/shard_map/ppermute | solution.py:21
  177.1 12.4 %collective-permute-start.43 = (bf16[96,384]{1,0:T(8,128)(2,1)S(1)}, bf16[96,384]{1,0:T(8,128)(2,1)S(1)}, u32[]{:S(2)}, u32[]{:S(2)}) collective-permute-start(bf16[96,384]{1,0:T(8,128)(2,1)S(1)} %get-tuple-element.70), channel_id=1, source_target_pairs={{0,65},{64,129},{128,193},{192,0},{1,64},{65,128},{129,192},{193,1... | collective-permute-start | bytes 221192 | tf_op jit(solution)/shard_map/ppermute | solution.py:21
  (26 other events, 317.3 us)

commit v2 on v1

--- a/solution.py
+++ b/solution.py
@@ -188,19 +188,7 @@
     lax.fori_loop(0, 3, n_step, 0)
 
 
-def half_body(coef, part, e0, e1, *refs):
-    s_of = inputs(refs)
-    s_of[2] = (refs[9].at[0], refs[10], refs[9].at[1])
-    out, acc = refs[11], refs[12]
-
-    def n_step(n, _):
-        cols = pl.ds(pl.multiple_of(n * 256, 256), 256)
-        acc[1, :, cols] = products(e1, s_of, (0, 1, 3, 2), cols)
-        acc[0, :, cols] = part[:, cols] + products(e0, s_of, (2,), cols)
-        return 0
-
-    lax.fori_loop(0, 3, n_step, 0)
-
+def mix_pair(coef, g, acc, before, out):
     tile_of = (0, 1, 3, 4)
     rows = 16
 
@@ -208,36 +196,64 @@
         a0 = pl.multiple_of(i * rows, rows)
 
         def tile(w, k):
-            return acc[w // 2, pl.ds((w % 2) * 192 + a0, rows), k * 128 : (k + 1) * 128]
+            return acc[pl.ds(w * 192 + a0, rows), k * 128 : (k + 1) * 128]
+
+        def put(s, lane, total):
+            part = pl.ds(s * 192 + a0, rows)
+            if before is not None:
+                total = total + before[part, lane : lane + 128]
+            out[part, lane : lane + 128] = total.astype(out.dtype)
 
         for v in range(4):
-            lane = (v // 2) * 384 + (v % 2) * 128
             totals = [None] * 4
-            for w in range(4):
+            for w in range(2):
                 for t in range(4):
                     x = tile(w, tile_of[t])
                     for s in range(4):
-                        idx = (v * 4 + s) * 16 + w * 4 + t
+                        idx = (v * 4 + s) * 16 + (2 * g + w) * 4 + t
                         d = coef[idx : idx + 1, :] * x
                         totals[s] = d if totals[s] is None else totals[s] + d
             for s in range(4):
-                out[pl.ds(s * 192 + a0, rows), lane : lane + 128] = totals[s].astype(BF16)
+                put(s, (v // 2) * 384 + (v % 2) * 128, totals[s])
         totals = [None] * 8
-        for w in range(4):
+        for w in range(2):
             for q in range(4):
                 x = tile(w, 2 if q < 2 else 5)
                 if q % 2:
                     x = pltpu.roll(x, 64, 1)
                 for vs in range(8):
-                    idx = 256 + vs * 16 + w * 4 + q
+                    idx = 256 + vs * 16 + (2 * g + w) * 4 + q
                     d = coef[idx : idx + 1, :] * x
                     totals[vs] = d if totals[vs] is None else totals[vs] + d
         for vs in range(8):
-            lane = (vs // 4) * 384 + 256
-            out[pl.ds((vs % 4) * 192 + a0, rows), lane : lane + 128] = totals[vs].astype(BF16)
+            put(vs % 4, (vs // 4) * 384 + 256, totals[vs])
         return 0
 
     lax.fori_loop(0, 192 // rows, a_step, 0)
+
+
+def mid_body(coef, part, e0, pair, near, out, acc):
+    def n_step(n, _):
+        cols = pl.ds(pl.multiple_of(n * 256, 256), 256)
+        acc[:, cols] = part[:, cols] + products(e0, {2: (pair.at[0], near, pair.at[1])}, (2,), cols)
+        return 0
+
+    lax.fori_loop(0, 3, n_step, 0)
+    mix_pair(coef, 0, acc, None, out)
+
+
+def half_body(coef, mown, e1, *refs):
+    s_of = inputs(refs)
+    s_of[2] = (refs[9].at[0], refs[10], refs[9].at[1])
+    out, acc = refs[11], refs[12]
+
+    def n_step(n, _):
+        cols = pl.ds(pl.multiple_of(n * 256, 256), 256)
+        acc[:, cols] = products(e1, s_of, (0, 1, 3, 2), cols)
+        return 0
+
+    lax.fori_loop(0, 3, n_step, 0)
+    mix_pair(coef, 1, acc, mown, out)
 
 
 def terms_of(js, rows, m_ref, mine, other, write):
@@ -462,13 +478,23 @@
     e1 = call(align_body, sds(4, 4, 384, 192), [e_oth, e_oth_s], nbytes=8 << 20)
     se = call(se_body, sds(4, 384, 768), [set_, sa, sc, sd, sb], nbytes=6 << 20)
     se_s = swap(se)
+    acc = [pltpu.VMEM((384, 768), F32)]
+    s_2 = [xf02, xf13]
+    mown = call(
+        mid_body,
+        sds(768, 768, dtype=F32),
+        [coef, part, e0, *s_2],
+        scratch=acc,
+        flops=2 * 384 * 768 * 768,
+        nbytes=6 << 20,
+    )
     mixed = call(
         half_body,
         sds(768, 768),
-        [coef, part, e0, e1, *s_in, xf02, xf13],
-        scratch=[pltpu.VMEM((2, 384, 768), F32)],
+        [coef, mown, e1, *s_in, *s_2],
+        scratch=acc,
         mib=20,
-        flops=2 * 384 * 768 * 3840,
+        flops=2 * 384 * 768 * 3072,
         nbytes=12 << 20,
     )
     qt, q2 = sds(4, 48, 768), sds(2, 4, 48, 768)

time: 198 us -> 205 us (1.035)
  the two profiles are of different devices: /device:TPU:54 before, /device:TPU:6 now
where the time goes in v2:
time: 205 us
  waiting for transfers between devices  111 us (54%)
  starting transfers between devices  68.5 us (33%)
  Pallas kernels  23.6 us (12%)
    ppermute x18, waiting for transfers between devices, flip_x(): return lax.ppermute(v, 'x', [(i, i ^ j) for i in range(4)])  59.4 us
    ppermute x13, starting transfers between devices, shift_z(): lax.ppermute(v, ('zl', 'zh'), [(_zi(z), _zi((z + k) % 8)) for z in range(...  31.7 us
    ppermute x10, waiting for transfers between devices, shift_y(): return lax.ppermute(v, 'y', [(i, (i + k) % 4) for i in range(4)])  27.7 us
    pallas_call x24, Pallas kernels, call(): pl.pallas_call(body, out_shape=outs, in_specs=[pl.BlockSpec(memory_space=...  23.6 us
    ppermute x13, waiting for transfers between devices, shift_z(): lax.ppermute(v, ('zl', 'zh'), [(_zi(z), _zi((z + k) % 8)) for z in range(...  22.6 us
    ppermute x18, starting transfers between devices, flip_x(): return lax.ppermute(v, 'x', [(i, i ^ j) for i in range(4)])  16.8 us
    ppermute x10, starting transfers between devices, shift_y(): return lax.ppermute(v, 'y', [(i, (i + k) % 4) for i in range(4)])  14.7 us
    ppermute x2, starting transfers between devices, flip_z(): return lax.ppermute(v, 'zl', [(i, i ^ j) for i in range(4)])  5.15 us
  transfers between devices with their start and end apart: 46, of which 27 were waited for; matrix products, arithmetic and copies ran while one was open for 0% of the time, Pallas kernels for 10%

profile of v2, /device:TPU:6, one launch (start us, length us, event | category | flops | bytes accessed | tf_op | source)
XLA Modules:
  0.0 205.1 jit_solution(16049065922216526452)
XLA Ops:
  1.4 3.1 %collective-permute-start.21 = (bf16[384,768]{1,0:T(8,128)(2,1)S(1)}, bf16[384,768]{1,0:T(8,128)(2,1)S(1)}, u32[]{:S(2)}, u32[]{:S(2)}) collective-permute-start(bf16[384,768]{1,0:T(8,128)(2,1)S(1)} %bitcast.7), channel_id=1, source_target_pairs={{0,12},{4,0},{8,4},{12,8},{1,13},{5,1},{9,5},{13,9},{2,14},{6,2},{... | collective-permute-start | bytes 1769480 | tf_op jit(solution)/shard_map/ppermute | solution.py:25
  4.5 12.6 %collective-permute-done.21.a.s1 = bf16[384,768]{1,0:T(8,128)(2,1)S(1)} collective-permute-done((bf16[384,768]{1,0:T(8,128)(2,1)S(1)}, bf16[384,768]{1,0:T(8,128)(2,1)S(1)}, u32[]{:S(2)}, u32[]{:S(2)}) %collective-permute-start.21) | collective-permute-done | bytes 589856 | tf_op jit(solution)/shard_map/ppermute | solution.py:25
  17.1 3.4 %collective-permute-done.22.b.s3 = bf16[384,768]{1,0:T(8,128)(2,1)S(1)} collective-permute-done((bf16[384,768]{1,0:T(8,128)(2,1)S(1)}, bf16[384,768]{1,0:T(8,128)(2,1)S(1)}, u32[]{:S(2)}, u32[]{:S(2)}) %collective-permute-start.22) | collective-permute-done | bytes 589856 | tf_op jit(solution)/shard_map/ppermute | solution.py:25
  24.5 3.3 %collective-permute-start.6 = (bf16[96,768]{1,0:T(8,128)(2,1)S(1)}, bf16[96,768]{1,0:T(8,128)(2,1)S(1)}, u32[]{:S(2)}, u32[]{:S(2)}) collective-permute-start(bf16[96,768]{1,0:T(8,128)(2,1)S(1)} %get-tuple-element.42), channel_id=1, source_target_pairs={{0,128},{64,192},{128,1},{192,65},{1,129},{65,193},{129,0},{193,64... | collective-permute-start | bytes 442376 | tf_op jit(solution)/shard_map/ppermute | solution.py:21
  27.8 3.1 %collective-permute-start.7 = (bf16[96,768]{1,0:T(8,128)(2,1)S(1)}, bf16[96,768]{1,0:T(8,128)(2,1)S(1)}, u32[]{:S(2)}, u32[]{:S(2)}) collective-permute-start(bf16[96,768]{1,0:T(8,128)(2,1)S(1)} %get-tuple-element.43), channel_id=1, source_target_pairs={{0,129},{64,193},{128,0},{192,64},{1,128},{65,192},{129,1},{193,65... | collective-permute-start | bytes 442376 | tf_op jit(solution)/shard_map/ppermute | solution.py:21
  31.8 3.7 %collective-permute-done.6.a = bf16[96,768]{1,0:T(8,128)(2,1)S(1)} collective-permute-done((bf16[96,768]{1,0:T(8,128)(2,1)S(1)}, bf16[96,768]{1,0:T(8,128)(2,1)S(1)}, u32[]{:S(2)}, u32[]{:S(2)}) %collective-permute-start.6) | collective-permute-done | bytes 147488 | tf_op jit(solution)/shard_map/ppermute | solution.py:21
  40.0 4.0 %collective-permute-start.16 = (bf16[384,384]{1,0:T(8,128)(2,1)S(1)}, bf16[384,384]{1,0:T(8,128)(2,1)S(1)}, u32[]{:S(2)}, u32[]{:S(2)}) collective-permute-start(bf16[384,384]{1,0:T(8,128)(2,1)S(1)} %bitcast.16), channel_id=1, source_target_pairs={{0,1},{64,65},{128,129},{192,193},{1,0},{65,64},{129,128},{193,192... | collective-permute-start | bytes 884744 | tf_op jit(solution)/shard_map/ppermute | solution.py:21
  46.5 9.6 %collective-permute-done.4.refs_0_ = bf16[192,768]{1,0:T(8,128)(2,1)S(1)} collective-permute-done((bf16[192,768]{1,0:T(8,128)(2,1)S(1)}, bf16[192,768]{1,0:T(8,128)(2,1)S(1)}, u32[]{:S(2)}, u32[]{:S(2)}) %collective-permute-start.4) | collective-permute-done | bytes 294944 | tf_op jit(solution)/shard_map/ppermute | solution.py:21
  56.8 3.9 %collective-permute-start.17 = (bf16[384,384]{1,0:T(8,128)(2,1)S(1)}, bf16[384,384]{1,0:T(8,128)(2,1)S(1)}, u32[]{:S(2)}, u32[]{:S(2)}) collective-permute-start(bf16[384,384]{1,0:T(8,128)(2,1)S(1)} %collective-permute-done.16.refs_0_), channel_id=1, source_target_pairs={{0,12},{4,0},{8,4},{12,8},{1,13},{5,1},{9,5},{13,9},{2,14},{6,2},{... | collective-permute-start | bytes 884744 | tf_op jit(solution)/shard_map/ppermute | solution.py:25
  64.1 8.3 %collective-permute-done.17.refs_1_ = bf16[384,384]{1,0:T(8,128)(2,1)S(1)} collective-permute-done((bf16[384,384]{1,0:T(8,128)(2,1)S(1)}, bf16[384,384]{1,0:T(8,128)(2,1)S(1)}, u32[]{:S(2)}, u32[]{:S(2)}) %collective-permute-start.17) | collective-permute-done | bytes 294944 | tf_op jit(solution)/shard_map/ppermute | solution.py:25
  73.9 2.9 %collective-permute-done.19.refs_3_ = bf16[384,384]{1,0:T(8,128)(2,1)S(1)} collective-permute-done((bf16[384,384]{1,0:T(8,128)(2,1)S(1)}, bf16[384,384]{1,0:T(8,128)(2,1)S(1)}, u32[]{:S(2)}, u32[]{:S(2)}) %collective-permute-start.19) | collective-permute-done | bytes 294944 | tf_op jit(solution)/shard_map/ppermute | solution.py:25
  82.5 17.2 %collective-permute-done.13.refs_8_ = bf16[192,768]{1,0:T(8,128)(2,1)S(1)} collective-permute-done((bf16[192,768]{1,0:T(8,128)(2,1)S(1)}, bf16[192,768]{1,0:T(8,128)(2,1)S(1)}, u32[]{:S(2)}, u32[]{:S(2)}) %collective-permute-start.13) | collective-permute-done | bytes 294944 | tf_op jit(solution)/shard_map/ppermute | solution.py:29
  101.9 4.3 %shard_map.55.coef = f32[384,128]{1,0:T(8,128)S(1)} custom-call(f32[4,4,12]{2,1,0:T(4,128)S(1)} %bitcast.18, s32[12]{0:T(128)S(1)} %copy-done.2, s32[12]{0:T(128)S(1)} %copy-done.3), custom_call_target="tpu_custom_call" | custom-call | bytes 1048576 | tf_op jit(solution)/shard_map/pallas_call | solution.py:42
  107.0 8.9 %collective-permute-done.9.refs_4_ = bf16[2,192,768]{2,1,0:T(8,128)(2,1)S(1)} collective-permute-done((bf16[2,192,768]{2,1,0:T(8,128)(2,1)S(1)}, bf16[2,192,768]{2,1,0:T(8,128)(2,1)S(1)}, u32[]{:S(2)}, u32[]{:S(2)}) %collective-permute-start.9) | collective-permute-done | bytes 589856 | tf_op jit(solution)/shard_map/ppermute | solution.py:29
  118.2 8.5 %collective-permute-done.15.near.refs_10_ = bf16[2,192,768]{2,1,0:T(8,128)(2,1)S(1)} collective-permute-done((bf16[2,192,768]{2,1,0:T(8,128)(2,1)S(1)}, bf16[2,192,768]{2,1,0:T(8,128)(2,1)S(1)}, u32[]{:S(2)}, u32[]{:S(2)}) %collective-permute-start.15) | collective-permute-done | bytes 589856 | tf_op jit(solution)/shard_map/ppermute | solution.py:29
  129.8 4.3 %shard_map.66.m_ref = bf16[768,768]{1,0:T(8,128)(2,1)S(1)} custom-call(f32[384,128]{1,0:T(8,128)S(1)} %shard_map.55.coef, f32[768,768]{1,0:T(8,128)S(1)} %shard_map.63.mown, bf16[4,4,384,192]{3,2,1,0:T(8,128)(2,1)S(1)} %shard_map.65.e1, bf16[192,768]{1,0:T(8,128)(2,1)S(1)} %get-tuple-element.39.refs_0_, bf16[2,192,768]{2,1,0:T(8,128)(2,1)S(1)} %shard_map.59.refs_1_, ...), custom_call_target="tpu_custom_call" | custom-call | flops 1811939328 | bytes 12582912 | tf_op jit(solution)/shard_map/pallas_call | solution.py:42
  136.3 3.2 %shard_map.70 = (bf16[2,4,48,768]{3,2,1,0:T(8,128)(2,1)S(1)}, bf16[2,4,48,768]{3,2,1,0:T(8,128)(2,1)S(1)}, bf16[4,48,768]{2,1,0:T(8,128)(2,1)S(1)}, bf16[4,48,76...) custom-call(bf16[768,768]{1,0:T(8,128)(2,1)S(1)} %shard_map.66.m_ref, ...), custom_call_target="tpu_custom_call" | custom-call | flops 2147483648 | bytes 8388608 | tf_op jit(solution)/shard_map/pallas_call | solution.py:42
  148.6 9.5 %collective-permute-done.26.m1.ra = bf16[2,4,48,768]{3,2,1,0:T(8,128)(2,1)S(1)} collective-permute-done((bf16[2,4,48,768]{3,2,1,0:T(8,128)(2,1)S(1)}, bf16[2,4,48,768]{3,2,1,0:T(8,128)(2,1)S(1)}, u32[]{:S(2)}, u32[]{:S(2)}) %collective-permute-start.26) | collective-permute-done | bytes 589856 | tf_op jit(solution)/shard_map/ppermute | solution.py:29
  158.7 4.5 %collective-permute-done.29.t3 = bf16[4,48,768]{2,1,0:T(8,128)(2,1)S(1)} collective-permute-done((bf16[4,48,768]{2,1,0:T(8,128)(2,1)S(1)}, bf16[4,48,768]{2,1,0:T(8,128)(2,1)S(1)}, u32[]{:S(2)}, u32[]{:S(2)}) %collective-permute-start.29) | collective-permute-done | bytes 294944 | tf_op jit(solution)/shard_map/ppermute | solution.py:29
  170.8 3.7 %collective-permute-start.33 = (bf16[96,768]{1,0:T(8,128)(2,1)S(1)}, bf16[96,768]{1,0:T(8,128)(2,1)S(1)}, u32[]{:S(2)}, u32[]{:S(2)}) collective-permute-start(bf16[96,768]{1,0:T(8,128)(2,1)S(1)} %get-tuple-element.58), channel_id=1, source_target_pairs={{0,128},{64,192},{128,0},{192,64},{1,129},{65,193},{129,1},{193,65... | collective-permute-start | bytes 442376 | tf_op jit(solution)/shard_map/ppermute | solution.py:33
  176.1 3.2 %collective-permute-done.36.t3 = bf16[4,48,768]{2,1,0:T(8,128)(2,1)S(1)} collective-permute-done((bf16[4,48,768]{2,1,0:T(8,128)(2,1)S(1)}, bf16[4,48,768]{2,1,0:T(8,128)(2,1)S(1)}, u32[]{:S(2)}, u32[]{:S(2)}) %collective-permute-start.36) | collective-permute-done | bytes 294944 | tf_op jit(solution)/shard_map/ppermute | solution.py:29
  180.3 3.0 %collective-permute-start.40 = (bf16[96,384]{1,0:T(8,128)(2,1)S(1)}, bf16[96,384]{1,0:T(8,128)(2,1)S(1)}, u32[]{:S(2)}, u32[]{:S(2)}) collective-permute-start(bf16[96,384]{1,0:T(8,128)(2,1)S(1)} %get-tuple-element.67), channel_id=1, source_target_pairs={{0,128},{64,192},{128,1},{192,65},{1,129},{65,193},{129,0},{193,64... | collective-permute-start | bytes 221192 | tf_op jit(solution)/shard_map/ppermute | solution.py:21
  183.3 3.3 %collective-permute-start.41 = (bf16[96,384]{1,0:T(8,128)(2,1)S(1)}, bf16[96,384]{1,0:T(8,128)(2,1)S(1)}, u32[]{:S(2)}, u32[]{:S(2)}) collective-permute-start(bf16[96,384]{1,0:T(8,128)(2,1)S(1)} %get-tuple-element.68), channel_id=1, source_target_pairs={{0,192},{64,1},{128,65},{192,129},{1,193},{65,0},{129,64},{193,128... | collective-permute-start | bytes 221192 | tf_op jit(solution)/shard_map/ppermute | solution.py:21
  188.3 3.3 %collective-permute-start.43 = (bf16[96,384]{1,0:T(8,128)(2,1)S(1)}, bf16[96,384]{1,0:T(8,128)(2,1)S(1)}, u32[]{:S(2)}, u32[]{:S(2)}) collective-permute-start(bf16[96,384]{1,0:T(8,128)(2,1)S(1)} %get-tuple-element.70), channel_id=1, source_target_pairs={{0,65},{64,129},{128,193},{192,0},{1,64},{65,128},{129,192},{193,1... | collective-permute-start | bytes 221192 | tf_op jit(solution)/shard_map/ppermute | solution.py:21
  (102 shorter events, 70.0 us)
Async XLA Ops:
  1.4 15.7 %collective-permute-start.21 = (bf16[384,768]{1,0:T(8,128)(2,1)S(1)}, bf16[384,768]{1,0:T(8,128)(2,1)S(1)}, u32[]{:S(2)}, u32[]{:S(2)}) collective-permute-start(bf16[384,768]{1,0:T(8,128)(2,1)S(1)} %bitcast.7), channel_id=1, source_target_pairs={{0,12},{4,0},{8,4},{12,8},{1,13},{5,1},{9,5},{13,9},{2,14},{6,2},{... | collective-permute-start | bytes 1769480 | tf_op jit(solution)/shard_map/ppermute | solution.py:25
  4.5 16.0 %collective-permute-start.22 = (bf16[384,768]{1,0:T(8,128)(2,1)S(1)}, bf16[384,768]{1,0:T(8,128)(2,1)S(1)}, u32[]{:S(2)}, u32[]{:S(2)}) collective-permute-start(bf16[384,768]{1,0:T(8,128)(2,1)S(1)} %bitcast.8), channel_id=1, source_target_pairs={{0,4},{4,8},{8,12},{12,0},{1,5},{5,9},{9,13},{13,1},{2,6},{6,10},{... | collective-permute-start | bytes 1769480 | tf_op jit(solution)/shard_map/ppermute | solution.py:25
  22.7 17.4 %collective-permute-start = (bf16[384,384]{1,0:T(8,128)(2,1)S(1)}, bf16[384,384]{1,0:T(8,128)(2,1)S(1)}, u32[]{:S(2)}, u32[]{:S(2)}) collective-permute-start(bf16[384,384]{1,0:T(8,128)(2,1)S(1)} %bitcast.13), channel_id=1, source_target_pairs={{0,12},{4,0},{8,4},{12,8},{1,13},{5,1},{9,5},{13,9},{2,14},{6,2},{... | collective-permute-start | bytes 884744 | tf_op jit(solution)/shard_map/ppermute | solution.py:25
  31.7 102.4 %collective-permute-start.25 = (bf16[4,384,768]{2,1,0:T(8,128)(2,1)S(1)}, bf16[4,384,768]{2,1,0:T(8,128)(2,1)S(1)}, u32[]{:S(2)}, u32[]{:S(2)}) collective-permute-start(bf16[4,384,768]{2,1,0:T(8,128)(2,1)S(1)} %shard_map.68.mine), channel_id=1, source_target_pairs={{0,2},{2,0},{1,3},{3,1},{4,6},{6,4},{5,7},{7,5},{8,10},{10,8},{9,1... | collective-permute-start | bytes 7077896 | tf_op jit(solution)/shard_map/ppermute | solution.py:37
  37.2 18.9 %collective-permute-start.4 = (bf16[192,768]{1,0:T(8,128)(2,1)S(1)}, bf16[192,768]{1,0:T(8,128)(2,1)S(1)}, u32[]{:S(2)}, u32[]{:S(2)}) collective-permute-start(bf16[192,768]{1,0:T(8,128)(2,1)S(1)} %get-tuple-element.40), channel_id=1, source_target_pairs={{0,193},{64,0},{128,64},{192,128},{1,192},{65,1},{129,65},{193,129... | collective-permute-start | bytes 884744 | tf_op jit(solution)/shard_map/ppermute | solution.py:21
  40.0 16.8 %collective-permute-start.16 = (bf16[384,384]{1,0:T(8,128)(2,1)S(1)}, bf16[384,384]{1,0:T(8,128)(2,1)S(1)}, u32[]{:S(2)}, u32[]{:S(2)}) collective-permute-start(bf16[384,384]{1,0:T(8,128)(2,1)S(1)} %bitcast.16), channel_id=1, source_target_pairs={{0,1},{64,65},{128,129},{192,193},{1,0},{65,64},{129,128},{193,192... | collective-permute-start | bytes 884744 | tf_op jit(solution)/shard_map/ppermute | solution.py:21
  44.0 17.3 %collective-permute-start.5 = (bf16[192,768]{1,0:T(8,128)(2,1)S(1)}, bf16[192,768]{1,0:T(8,128)(2,1)S(1)}, u32[]{:S(2)}, u32[]{:S(2)}) collective-permute-start(bf16[192,768]{1,0:T(8,128)(2,1)S(1)} %get-tuple-element.41), channel_id=1, source_target_pairs={{0,64},{64,128},{128,192},{192,1},{1,65},{65,129},{129,193},{193,0... | collective-permute-start | bytes 884744 | tf_op jit(solution)/shard_map/ppermute | solution.py:21
  45.5 16.8 %collective-permute-start.8 = (bf16[192,768]{1,0:T(8,128)(2,1)S(1)}, bf16[192,768]{1,0:T(8,128)(2,1)S(1)}, u32[]{:S(2)}, u32[]{:S(2)}) collective-permute-start(bf16[192,768]{1,0:T(8,128)(2,1)S(1)} %get-tuple-element.39.refs_0_), channel_id=1, source_target_pairs={{0,16},{16,0},{32,48},{48,32},{1,17},{17,1},{33,49},{49,33},{2,18}... | collective-permute-start | bytes 884744 | tf_op jit(solution)/shard_map/ppermute | solution.py:29
  56.1 44.5 %collective-permute-start.3 = (bf16[4,384,384]{2,1,0:T(8,128)(2,1)S(1)}, bf16[4,384,384]{2,1,0:T(8,128)(2,1)S(1)}, u32[]{:S(2)}, u32[]{:S(2)}) collective-permute-start(bf16[4,384,384]{2,1,0:T(8,128)(2,1)S(1)} %shard_map.56.mine), channel_id=1, source_target_pairs={{0,2},{2,0},{1,3},{3,1},{4,6},{6,4},{5,7},{7,5},{8,10},{10,8},{9,1... | collective-permute-start | bytes 3538952 | tf_op jit(solution)/shard_map/ppermute | solution.py:37
  56.8 15.6 %collective-permute-start.17 = (bf16[384,384]{1,0:T(8,128)(2,1)S(1)}, bf16[384,384]{1,0:T(8,128)(2,1)S(1)}, u32[]{:S(2)}, u32[]{:S(2)}) collective-permute-start(bf16[384,384]{1,0:T(8,128)(2,1)S(1)} %collective-permute-done.16.refs_0_), channel_id=1, source_target_pairs={{0,12},{4,0},{8,4},{12,8},{1,13},{5,1},{9,5},{13,9},{2,14},{6,2},{... | collective-permute-start | bytes 884744 | tf_op jit(solution)/shard_map/ppermute | solution.py:25
  62.3 14.5 %collective-permute-start.19 = (bf16[384,384]{1,0:T(8,128)(2,1)S(1)}, bf16[384,384]{1,0:T(8,128)(2,1)S(1)}, u32[]{:S(2)}, u32[]{:S(2)}) collective-permute-start(bf16[384,384]{1,0:T(8,128)(2,1)S(1)} %collective-permute-done.16.refs_0_), channel_id=1, source_target_pairs={{0,4},{4,8},{8,12},{12,0},{1,5},{5,9},{9,13},{13,1},{2,6},{6,10},{... | collective-permute-start | bytes 884744 | tf_op jit(solution)/shard_map/ppermute | solution.py:25
  76.9 22.8 %collective-permute-start.12 = (bf16[2,192,768]{2,1,0:T(8,128)(2,1)S(1)}, bf16[2,192,768]{2,1,0:T(8,128)(2,1)S(1)}, u32[]{:S(2)}, u32[]{:S(2)}) collective-permute-start(bf16[2,192,768]{2,1,0:T(8,128)(2,1)S(1)} %shard_map.59.refs_1_), channel_id=1, source_target_pairs={{0,48},{16,32},{32,16},{48,0},{1,49},{17,33},{33,17},{49,1},{2,50}... | collective-permute-start | bytes 1769480 | tf_op jit(solution)/shard_map/ppermute | solution.py:29
  80.4 48.7 %collective-permute-start.20 = (bf16[4,384,384]{2,1,0:T(8,128)(2,1)S(1)}, bf16[4,384,384]{2,1,0:T(8,128)(2,1)S(1)}, u32[]{:S(2)}, u32[]{:S(2)}) collective-permute-start(bf16[4,384,384]{2,1,0:T(8,128)(2,1)S(1)} %shard_map.64.mine), channel_id=1, source_target_pairs={{0,2},{2,0},{1,3},{3,1},{4,6},{6,4},{5,7},{7,5},{8,10},{10,8},{9,1... | collective-permute-start | bytes 3538952 | tf_op jit(solution)/shard_map/ppermute | solution.py:37
  80.4 19.3 %collective-permute-start.13 = (bf16[192,768]{1,0:T(8,128)(2,1)S(1)}, bf16[192,768]{1,0:T(8,128)(2,1)S(1)}, u32[]{:S(2)}, u32[]{:S(2)}) collective-permute-start(bf16[192,768]{1,0:T(8,128)(2,1)S(1)} %shard_map.60.refs_2_), channel_id=1, source_target_pairs={{0,48},{16,32},{32,16},{48,0},{1,49},{17,33},{33,17},{49,1},{2,50}... | collective-permute-start | bytes 884744 | tf_op jit(solution)/shard_map/ppermute | solution.py:29
  99.7 16.2 %collective-permute-start.9 = (bf16[2,192,768]{2,1,0:T(8,128)(2,1)S(1)}, bf16[2,192,768]{2,1,0:T(8,128)(2,1)S(1)}, u32[]{:S(2)}, u32[]{:S(2)}) collective-permute-start(bf16[2,192,768]{2,1,0:T(8,128)(2,1)S(1)} %shard_map.59.refs_1_), channel_id=1, source_target_pairs={{0,16},{16,0},{32,48},{48,32},{1,17},{17,1},{33,49},{49,33},{2,18}... | collective-permute-start | bytes 1769480 | tf_op jit(solution)/shard_map/ppermute | solution.py:29
  99.7 18.4 %collective-permute-start.14 = (bf16[2,192,768]{2,1,0:T(8,128)(2,1)S(1)}, bf16[2,192,768]{2,1,0:T(8,128)(2,1)S(1)}, u32[]{:S(2)}, u32[]{:S(2)}) collective-permute-start(bf16[2,192,768]{2,1,0:T(8,128)(2,1)S(1)} %shard_map.62), channel_id=1, source_target_pairs={{0,48},{16,32},{32,16},{48,0},{1,49},{17,33},{33,17},{49,1},{2,50}... | collective-permute-start | bytes 1769480 | tf_op jit(solution)/shard_map/ppermute | solution.py:29
  100.6 26.1 %collective-permute-start.15 = (bf16[2,192,768]{2,1,0:T(8,128)(2,1)S(1)}, bf16[2,192,768]{2,1,0:T(8,128)(2,1)S(1)}, u32[]{:S(2)}, u32[]{:S(2)}) collective-permute-start(bf16[2,192,768]{2,1,0:T(8,128)(2,1)S(1)} %collective-permute-done.12.refs_7_), channel_id=1, source_target_pairs={{0,16},{16,0},{32,48},{48,32},{1,17},{17,1},{33,49},{49,33},{2,18}... | collective-permute-start | bytes 1769480 | tf_op jit(solution)/shard_map/ppermute | solution.py:29
  139.5 18.5 %collective-permute-start.26 = (bf16[2,4,48,768]{3,2,1,0:T(8,128)(2,1)S(1)}, bf16[2,4,48,768]{3,2,1,0:T(8,128)(2,1)S(1)}, u32[]{:S(2)}, u32[]{:S(2)}) collective-permute-start(bf16[2,4,48,768]{3,2,1,0:T(8,128)(2,1)S(1)} %get-tuple-element.46), channel_id=1, source_target_pairs={{0,16},{16,0},{32,48},{48,32},{1,17},{17,1},{33,49},{49,33},{2,18}... | collective-permute-start | bytes 1769480 | tf_op jit(solution)/shard_map/ppermute | solution.py:29
  140.9 17.9 %collective-permute-start.30 = (bf16[2,4,48,768]{3,2,1,0:T(8,128)(2,1)S(1)}, bf16[2,4,48,768]{3,2,1,0:T(8,128)(2,1)S(1)}, u32[]{:S(2)}, u32[]{:S(2)}) collective-permute-start(bf16[2,4,48,768]{3,2,1,0:T(8,128)(2,1)S(1)} %get-tuple-element.52), channel_id=1, source_target_pairs={{0,48},{16,32},{32,16},{48,0},{1,49},{17,33},{33,17},{49,1},{2,50}... | collective-permute-start | bytes 1769480 | tf_op jit(solution)/shard_map/ppermute | solution.py:29
  146.2 17.0 %collective-permute-start.29 = (bf16[4,48,768]{2,1,0:T(8,128)(2,1)S(1)}, bf16[4,48,768]{2,1,0:T(8,128)(2,1)S(1)}, u32[]{:S(2)}, u32[]{:S(2)}) collective-permute-start(bf16[4,48,768]{2,1,0:T(8,128)(2,1)S(1)} %get-tuple-element.51), channel_id=1, source_target_pairs={{0,48},{16,32},{32,16},{48,0},{1,49},{17,33},{33,17},{49,1},{2,50}... | collective-permute-start | bytes 884744 | tf_op jit(solution)/shard_map/ppermute | solution.py:29
  146.3 16.9 %collective-permute-start.31 = (bf16[4,48,768]{2,1,0:T(8,128)(2,1)S(1)}, bf16[4,48,768]{2,1,0:T(8,128)(2,1)S(1)}, u32[]{:S(2)}, u32[]{:S(2)}) collective-permute-start(bf16[4,48,768]{2,1,0:T(8,128)(2,1)S(1)} %get-tuple-element.53), channel_id=1, source_target_pairs={{0,16},{16,0},{32,48},{48,32},{1,17},{17,1},{33,49},{49,33},{2,18}... | collective-permute-start | bytes 884744 | tf_op jit(solution)/shard_map/ppermute | solution.py:29
  166.1 13.2 %collective-permute-start.36 = (bf16[4,48,768]{2,1,0:T(8,128)(2,1)S(1)}, bf16[4,48,768]{2,1,0:T(8,128)(2,1)S(1)}, u32[]{:S(2)}, u32[]{:S(2)}) collective-permute-start(bf16[4,48,768]{2,1,0:T(8,128)(2,1)S(1)} %get-tuple-element.62), channel_id=1, source_target_pairs={{0,48},{16,32},{32,16},{48,0},{1,49},{17,33},{33,17},{49,1},{2,50}... | collective-permute-start | bytes 884744 | tf_op jit(solution)/shard_map/ppermute | solution.py:29
  170.8 17.5 %collective-permute-start.33 = (bf16[96,768]{1,0:T(8,128)(2,1)S(1)}, bf16[96,768]{1,0:T(8,128)(2,1)S(1)}, u32[]{:S(2)}, u32[]{:S(2)}) collective-permute-start(bf16[96,768]{1,0:T(8,128)(2,1)S(1)} %get-tuple-element.58), channel_id=1, source_target_pairs={{0,128},{64,192},{128,0},{192,64},{1,129},{65,193},{129,1},{193,65... | collective-permute-start | bytes 442376 | tf_op jit(solution)/shard_map/ppermute | solution.py:33
  180.3 14.2 %collective-permute-start.40 = (bf16[96,384]{1,0:T(8,128)(2,1)S(1)}, bf16[96,384]{1,0:T(8,128)(2,1)S(1)}, u32[]{:S(2)}, u32[]{:S(2)}) collective-permute-start(bf16[96,384]{1,0:T(8,128)(2,1)S(1)} %get-tuple-element.67), channel_id=1, source_target_pairs={{0,128},{64,192},{128,1},{192,65},{1,129},{65,193},{129,0},{193,64... | collective-permute-start | bytes 221192 | tf_op jit(solution)/shard_map/ppermute | solution.py:21
  (26 other events, 314.6 us)
